TPU v7x, 8 devices: a whole 2x2x1 slice. The times are simulated.
8 devices in a mesh: col: 2 (over z, y), row: 4 (over x, core).
Axes of the slice: x: 2, y: 2, z: 1, core: 2. Of those that a mesh axis runs over, the one named last changes fastest.
Arguments:
- t_amps: float32 [256, 6400], P('row', 'col')
- denoms: float32 [256, 6400], P('row', 'col')
- v_oovv: bfloat16 [256, 6400], P('row', 'col')
- v_vvvv: bfloat16 [6400, 6400], P('row', 'col')
- v_oooo: bfloat16 [256, 256], replicated
- w_direct: bfloat16 [1280, 1280], P(None, 'col')
- w_exch: bfloat16 [1280, 1280], P(None, 'col')
Outputs:
- output: float32 [256, 6400], P('row', 'col')
All inputs are finite; a program needn't handle non-finite values.
Results may differ from a plain program's by a relative error of at most 0.001.
Values are sent between devices in bfloat16 or wider.
A program may use at most 1 GiB of HBM per device.

v0:
```python
import math
import jax
import jax.numpy as jnp
from jax import lax
from jax.sharding import PartitionSpec as P


def solution(mesh):
    n_row = mesh.shape["row"]
    n_col = mesh.shape["col"]
    amp_spec = P("row", "col")
    wide_spec = P(None, "col")

    def local_sweep(t_blk, d_blk, oovv_blk, vvvv_blk, oooo_full, wd_blk, wx_blk):
        rows_dev, cols_dev = t_blk.shape
        n_occ = math.isqrt(oooo_full.shape[0])
        n_virt = wd_blk.shape[0] // n_occ
        occ_row = n_occ // n_row
        occ_col = n_occ // n_col
        t_half = t_blk.astype(jnp.bfloat16)
        t_rows = lax.all_gather(t_half, "col", axis=1, tiled=True)
        t_ladder = lax.all_to_all(t_rows, "row", 1, 0, tiled=True)
        ladder_part = jnp.dot(t_ladder, vvvv_blk, preferred_element_type=jnp.float32)
        t_cols = lax.all_gather(t_half, "row", axis=0, tiled=True)
        x_part = lax.dot_general(oovv_blk, t_cols, (((1,), (1,)), ((), ())), preferred_element_type=jnp.float32)
        x_rows = lax.psum(x_part, "col")
        row_idx = lax.axis_index("row")
        oooo_rows = lax.dynamic_slice_in_dim(oooo_full, row_idx * rows_dev, rows_dev, axis=0)
        hole_mat = (oooo_rows.astype(jnp.float32) + 0.5 * x_rows).astype(jnp.bfloat16)
        hole_part = lax.dot_general(hole_mat, t_half, (((0,), (0,)), ((), ())), preferred_element_type=jnp.float32)
        ladder_sum = lax.psum_scatter(ladder_part + hole_part, "row", scatter_dimension=0, tiled=True)
        t_four = t_rows.reshape(occ_row, n_occ, n_virt, n_virt)
        direct_term = jnp.einsum("ikac,kcjb->ijab", t_four, wd_blk.reshape(n_occ, n_virt, occ_col, n_virt), preferred_element_type=jnp.float32)
        exch_term = jnp.einsum("ikcb,kcja->ijab", t_four, wx_blk.reshape(n_occ, n_virt, occ_col, n_virt), preferred_element_type=jnp.float32)
        ph_back = lax.all_to_all(direct_term - exch_term, "col", 2, 1, tiled=True)
        swap_row = lax.all_to_all(ph_back, "row", 1, 0, tiled=True)
        swap_both = lax.all_to_all(swap_row, "col", 3, 2, tiled=True)
        ph_sym = (ph_back + swap_both.transpose(1, 0, 3, 2)).reshape(rows_dev, cols_dev)
        residual = oovv_blk.astype(jnp.float32) + ladder_sum + ph_sym
        return residual / d_blk

    return jax.shard_map(local_sweep, mesh=mesh, in_specs=(amp_spec, amp_spec, amp_spec, amp_spec, P(), wide_spec, wide_spec), out_specs=amp_spec, check_vma=False)
```

profile of v0, /device:TPU:0, one launch (start us, length us, event | category | flops | bytes accessed | tf_op | source)
XLA Modules:
  0.0 162.5 jit_solution(514629439321267136)
XLA Ops:
  6.5 0.0 all-gather.2.cloned.1.call-start
  6.5 1.9 %convert_element_type.13 = bf16[64,3200]{1,0:T(8,128)(2,1)} convert(f32[64,3200]{1,0:T(8,128)} %param.7) | non-fusion elementwise | flops 204800 | bytes 1228800 | tf_op jit(solution)/shard_map/convert_element_type | solution.py:20
  8.5 0.0 all-gather.2.cloned.1.call-update
  8.5 13.5 %all_gather.6 = bf16[64,6400]{1,0:T(8,128)(2,1)S(1)} all-gather(bf16[64,3200]{1,0:T(8,128)(2,1)} %convert_element_type.13), channel_id=1, replica_groups=mesh['col'=2,'row'=4] {'col'}, dimensions={1}, use_global_device_ids=true | all-gather | bytes 1228800 | tf_op jit(solution)/shard_map/all_gather | solution.py:21
  22.0 1.0 all_to_all.53
  23.0 0.0 copy-start.1
  23.0 1.0 copy.26
  24.0 3.5 %all-to-all-start = ((bf16[64,4,1600]{2,0,1:T(8,128)(2,1)}), bf16[64,4,1600]{2,0,1:T(8,128)(2,1)S(1)}, u32[]{:S(2)}, u32[]{:S(2)}) async-start(bf16[64,4,1600]{2,0,1:T(8,128)(2,1)} %copy.26), calls=%async_computation | async-start | bytes 1703936 | tf_op jit(solution)/shard_map/all_to_all | solution.py:22
  27.5 0.0 all-reduce.2.cloned.1.call-start
  27.6 1.2 all-gather.2.cloned.1.call-done
  28.8 0.0 copy-done.1
  28.8 2.7 %fusion.18 = f32[64,256]{1,0:T(8,128)} fusion(bf16[64,3200]{1,0:T(8,128)(2,1)S(1)} %copy-done.1, bf16[256,3200]{1,0:T(8,128)(2,1)} %all-gather.2.cloned.1.call-done), kind=kOutput, calls=%fused_computation.17 | convolution fusion | flops 104857600 | bytes 2113536 | tf_op jit(solution)/shard_map/dot_general | solution.py:25
  31.4 0.0 all-reduce.2.cloned.1.call-update
  31.5 0.0 reduce-scatter.2.cloned.1.call-start
  31.5 8.1 %all-to-all-done = bf16[64,4,1600]{2,0,1:T(8,128)(2,1)S(1)} async-done(((bf16[64,4,1600]{2,0,1:T(8,128)(2,1)}), bf16[64,4,1600]{2,0,1:T(8,128)(2,1)S(1)}, u32[]{:S(2)}, u32[]{:S(2)}) %all-to-all-start) | async-done | bytes 819232 | tf_op jit(solution)/shard_map/all_to_all | solution.py:22
  39.6 0.0 copy-start
  39.6 8.9 %fusion.17 = f32[256,3200]{1,0:T(8,128)} fusion(bf16[256,1600]{1,0:T(8,128)(2,1)S(1)} %bitcast.54, bf16[1600,3200]{1,0:T(8,128)(2,1)} %param.10), kind=kOutput, calls=%fused_computation.16 | convolution fusion | flops 2621440000 | bytes 14336000 | tf_op jit(solution)/shard_map/dot_general | solution.py:23
  48.5 0.0 all-reduce.2.cloned.1.call-done
  48.5 0.0 copy-done
  48.5 4.3 %convolution_add_fusion = f32[256,3200]{1,0:T(8,128)} fusion(f32[256,3200]{1,0:T(8,128)} %fusion.17, bf16[64,3200]{1,0:T(8,128)(2,1)S(1)} %copy-done, f32[64,256]{1,0:T(8,128)} %all-reduce.2.cloned.1.call-done, bf16[256,256]{1,0:T(8,128)(2,1)} %param.11, s32[]{:T(128)S(6)} %select_n.3), kind=kOutput, calls=%fused_computation | convolution fusion | flops 105742336 | bytes 7061508 | tf_op jit(solution)/shard_map/dot_general | solution.py:30
  52.8 0.0 reduce-scatter.2.cloned.1.call-update
  52.8 0.0 copy-start.2
  52.8 3.1 %reshape.20 = bf16[4,16,80,80,1]{3,2,1,0,4:T(8,128)(2,1)} reshape(bf16[64,6400]{1,0:T(8,128)(2,1)S(1)} %all_gather.6) | data formatting | bytes 1638400 | tf_op jit(solution)/shard_map/reshape | solution.py:32
  55.9 0.0 copy-done.2
  55.9 3.7 %reshape.17 = bf16[16,80,8,80]{3,2,1,0:T(8,128)(2,1)} reshape(bf16[1280,640]{1,0:T(8,128)(2,1)S(1)} %copy-done.2) | data formatting | bytes 3276800 | tf_op jit(solution)/shard_map/reshape | solution.py:34
  59.7 4.1 %reshape.15 = bf16[16,80,8,80]{3,2,1,0:T(8,128)(2,1)S(1)} reshape(bf16[1280,640]{1,0:T(8,128)(2,1)} %param.12) | data formatting | bytes 3276800 | tf_op jit(solution)/shard_map/reshape | solution.py:33
  63.7 0.0 copy-start.3
  63.7 3.3 %fusion.4 = f32[4,8,80,80]{2,3,0,1:T(8,128)S(1)} fusion(bf16[4,16,80,80,1]{3,2,1,0,4:T(8,128)(2,1)} %reshape.20, bf16[16,80,8,80,1]{3,2,1,0,4:T(8,128)(2,1)} %bitcast.53), kind=kOutput, calls=%fused_computation.6 | convolution fusion | flops 524288000 | bytes 3276800 | tf_op jit(solution)/shard_map/ikcb,kcja->ijab/dot_general | solution.py:34
  67.0 0.0 copy-done.3
  67.0 2.6 %fusion.10 = f32[4,8,80,80]{2,3,0,1:T(8,128)} fusion(f32[4,8,80,80]{2,3,0,1:T(8,128)S(1)} %fusion.4, bf16[4,16,80,80,1]{3,2,1,0,4:T(8,128)(2,1)S(1)} %copy-done.3, bf16[16,80,8,80,1]{3,2,1,0,4:T(8,128)(2,1)S(1)} %bitcast.52), kind=kOutput, calls=%fused_computation.8 | convolution fusion | flops 524492800 | bytes 4096000 | tf_op jit(solution)/shard_map/ikac,kcjb->ijab/dot_general | solution.py:33
  69.6 2.1 %copy.30 = f32[4,8,80,80]{3,0,1,2:T(4,128)S(1)} copy(f32[4,8,80,80]{2,3,0,1:T(8,128)} %fusion.10) | data formatting | bytes 1638400 | tf_op jit(solution)/shard_map/sub | solution.py:35
  71.7 18.9 %all_to_all.73 = f32[4,8,80,80]{3,0,1,2:T(4,128)S(1)} all-to-all(f32[4,8,80,80]{3,0,1,2:T(4,128)S(1)} %copy.30), channel_id=1, replica_groups=mesh['col'=2,'row'=4] {'col'}, dimensions={2} | all-to-all | bytes 1638400 | tf_op jit(solution)/shard_map/all_to_all | solution.py:35
  90.7 0.8 copy.31
  91.4 0.1 copy.32
  91.5 0.1 copy.33
  91.7 19.7 %all_to_all.74 = f32[4,16,40,80]{3,2,0,1:T(8,128)S(1)} all-to-all(f32[4,16,40,80]{3,2,0,1:T(8,128)S(1)} %copy.33), channel_id=1, replica_groups=mesh['col'=2,'row'=4] {'row'}, dimensions={1} | all-to-all | bytes 1638400 | tf_op jit(solution)/shard_map/all_to_all | solution.py:36
  111.3 0.1 copy.35
  111.5 3.3 %copy.36 = f32[16,4,40,80]{2,1,0,3:T(4,128)} copy(f32[16,4,40,80]{3,2,1,0:T(8,128)S(1)} %bitcast.51) | data formatting | bytes 1638400 | tf_op jit(solution)/shard_map/all_to_all | solution.py:36
  114.7 5.0 %reshape.25 = f32[2,1,102400]{2,1,0:T(1,128)S(1)} reshape(f32[80,16,4,40]{3,2,1,0:T(4,128)} %bitcast.48) | data formatting | bytes 1638400
  119.8 13.5 %all_to_all.75 = f32[2,1,102400]{2,1,0:T(1,128)S(1)} all-to-all(f32[2,1,102400]{2,1,0:T(1,128)S(1)} %reshape.25), channel_id=1, replica_groups=mesh['col'=2,'row'=4] {'col'}, dimensions={0} | all-to-all | bytes 1638400 | tf_op jit(solution)/shard_map/all_to_all | solution.py:37
  133.2 0.5 broadcast
  133.8 3.2 %reduce = f32[2,102400]{1,0:T(2,128)S(1)} reduce(f32[2,1,102400]{2,1,0:T(1,128)S(1)} %all_to_all.75, f32[]{:T(128)} %broadcast), dimensions={1}, to_apply=%all_to_all.65.reduce_sub_computation | reduce | bytes 1638404 | tf_op jit(solution)/shard_map/all_to_all | solution.py:37
  137.0 5.6 %reshape.26 = f32[80,16,4,40]{3,2,1,0:T(4,128)} reshape(f32[2,102400]{1,0:T(2,128)S(1)} %reduce) | data formatting | bytes 1638400
  142.6 5.3 %copy.64 = f32[16,4,40,2,40]{2,3,4,1,0:T(2,128)} copy(f32[16,4,40,2,40]{2,1,0,4,3:T(4,128)} %bitcast.46) | data formatting | bytes 1638400 | tf_op jit(solution)/shard_map/all_to_all | solution.py:37
  147.9 2.9 %all_to_all.68 = f32[16,4,80,40]{2,3,1,0:T(8,128)S(1)} reshape(f32[16,4,2,40,40]{3,2,4,1,0:T(2,128)} %bitcast.47) | data formatting | bytes 1638400 | tf_op jit(solution)/shard_map/all_to_all | solution.py:37
  150.8 1.2 bitcast_add_fusion
  151.9 0.0 copy-start.4
  151.9 1.8 %reshape.18 = f32[64,3200]{1,0:T(8,128)S(1)} reshape(f32[4,16,40,80]{3,2,1,0:T(8,128)} %bitcast_add_fusion) | data formatting | bytes 1638400 | tf_op jit(solution)/shard_map/reshape | solution.py:38
  153.8 0.0 reduce-scatter.2.cloned.1.call-done
  153.8 0.0 copy-done.4
  153.8 2.2 %add_divide_fusion = f32[64,3200]{1,0:T(8,128)} fusion(f32[64,3200]{1,0:T(8,128)S(1)} %copy-done.4, f32[64,3200]{1,0:T(8,128)S(1)} %reshape.18, f32[64,3200]{1,0:T(8,128)} %reduce-scatter.2.cloned.1.call-done, bf16[64,3200]{1,0:T(8,128)(2,1)S(1)} %copy-done.1), kind=kLoop, calls=%fused_computation.10 | loop fusion | flops 819200 | bytes 3686400 | tf_op jit(solution)/shard_map/div | solution.py:40
Async XLA Ops:
  6.5 22.2 %all-gather.2.cloned.1.call-start = ((), (), s32[]{:S(2)}) async-start(), calls=%async_computation.5 | async-start | bytes 2048000 | tf_op jit(solution)/shard_map/all_gather | solution.py:24
  23.0 5.7 %copy-start.1 = (bf16[64,3200]{1,0:T(8,128)(2,1)S(1)}, bf16[64,3200]{1,0:T(8,128)(2,1)}, u32[]{:S(2)}) copy-start(bf16[64,3200]{1,0:T(8,128)(2,1)} %param.9) | copy-start | bytes 1228804
  24.0 15.6 %all-to-all-start = ((bf16[64,4,1600]{2,0,1:T(8,128)(2,1)}), bf16[64,4,1600]{2,0,1:T(8,128)(2,1)S(1)}, u32[]{:S(2)}, u32[]{:S(2)}) async-start(bf16[64,4,1600]{2,0,1:T(8,128)(2,1)} %copy.26), calls=%async_computation | async-start | bytes 1703936 | tf_op jit(solution)/shard_map/all_to_all | solution.py:22
  27.5 20.9 %all-reduce.2.cloned.1.call-start = ((), (), s32[]{:S(2)}) async-start(), calls=%async_computation.6 | async-start | bytes 131072 | tf_op jit(solution)/shard_map/psum | solution.py:26
  31.5 122.3 %reduce-scatter.2.cloned.1.call-start = ((), (), s32[]{:S(2)}) async-start(), calls=%async_computation.7 | async-start | bytes 4096000 | tf_op jit(solution)/shard_map/reduce_scatter | solution.py:31
  39.6 8.9 %copy-start = (bf16[64,3200]{1,0:T(8,128)(2,1)S(1)}, bf16[64,3200]{1,0:T(8,128)(2,1)}, u32[]{:S(2)}) copy-start(bf16[64,3200]{1,0:T(8,128)(2,1)} %convert_element_type.13) | copy-start | bytes 1228804
  52.8 3.1 %copy-start.2 = (bf16[1280,640]{1,0:T(8,128)(2,1)S(1)}, bf16[1280,640]{1,0:T(8,128)(2,1)}, u32[]{:S(2)}) copy-start(bf16[1280,640]{1,0:T(8,128)(2,1)} %param.13) | copy-start | bytes 4915204
  63.7 3.3 %copy-start.3 = (bf16[4,16,80,80,1]{3,2,1,0,4:T(8,128)(2,1)S(1)}, bf16[4,16,80,80,1]{3,2,1,0,4:T(8,128)(2,1)}, u32[]{:S(2)}) copy-start(bf16[4,16,80,80,1]{3,2,1,0,4:T(8,128)(2,1)} %reshape.20) | copy-start | bytes 2457604
  151.9 1.8 %copy-start.4 = (f32[64,3200]{1,0:T(8,128)S(1)}, f32[64,3200]{1,0:T(8,128)}, u32[]{:S(2)}) copy-start(f32[64,3200]{1,0:T(8,128)} %param.8) | copy-start | bytes 2457604
Sparse Core Ops, SparseCore 0:
  8.9 19.8 all-gather.1
  31.6 15.9 all-reduce.1
  52.9 32.9 reduce-scatter.1
where the time goes:
time: 163 us; the launch traced here: 162 us
  blocking collectives  65.6 us (40%)
  local copies, waits for them, and re-layouts  40.5 us (25%)
  matrix products  21.7 us (13%)
  between operations  13.3 us (8%)
  waiting for transfers between devices  9.35 us (6%)
  other arithmetic  8.54 us (5%)
  starting transfers between devices  3.58 us (2%)
    all_to_all x1, blocking collectives, local_sweep(): swap_row = lax.all_to_all(ph_back, 'row', 1, 0, tiled=True)  19.7 us
    all_to_all x1, blocking collectives, local_sweep(): ph_back = lax.all_to_all(direct_term - exch_term, 'col', 2, 1, tiled=True)  18.9 us
    all_gather x1, blocking collectives, local_sweep(): t_rows = lax.all_gather(t_half, 'col', axis=1, tiled=True)  13.5 us
    all_to_all x1, blocking collectives, local_sweep(): swap_both = lax.all_to_all(swap_row, 'col', 3, 2, tiled=True)  13.5 us
    unnamed x12, local copies, waits for them, and re-layouts  10.7 us
    dot_general x1, matrix products, local_sweep(): jnp.dot(t_ladder, vvvv_blk, preferred_element_type=jnp.float32)  8.86 us
    all_to_all x3, local copies, waits for them, and re-layouts, local_sweep(): swap_both = lax.all_to_all(swap_row, 'col', 3, 2, tiled=True)  8.63 us
    all_to_all x1, waiting for transfers between devices, local_sweep(): t_ladder = lax.all_to_all(t_rows, 'row', 1, 0, tiled=True)  8.11 us
  transfers between devices with their start and end apart: 4, of which 2 were waited for; matrix products, arithmetic and copies ran while one was open for 36% of the time, Pallas kernels for 0%

commit v1 on v0

v1 whole, which is shorter than its diff:
```python
import functools

import jax
import jax.numpy as jnp
from jax import lax
from jax.experimental import pallas as pl
from jax.experimental.pallas import tpu as pltpu
from jax.sharding import PartitionSpec as P

MESH = pl.DeviceIdType.MESH
F32 = jnp.float32
BF16 = jnp.bfloat16

OCC = 16
VIRT = 80
ROWS = 64
COLS = 3200
KPAD = 1664
WIDE = 640
NCH = COLS // WIDE
ZT = 72
ZS = 40

T_X, T_Y, T_P, T_FWD, R_P, R_2, R_3, G_P = 0, 2, 4, 5, 7, 8, 10, 12
E_D, L_D, E_X, L_X, O_D, F_Y, G_Y, X_Y, M_1, M_2, M_3 = 16, 21, 26, 31, 36, 41, 46, 51, 52, 53, 54
N_SEM = 55


def split_segments(parts, lane):
    out = []
    for q in range(8):
        m, s = divmod(80 * q, 128)
        seg = parts[m]
        if s:
            seg = pltpu.roll(seg, 128 - s, axis=1)
            if s + 80 > 128:
                seg = jnp.where(lane < 128 - s, seg, pltpu.roll(parts[m + 1], 128 - s, axis=1))
        out.append(jnp.where(lane < 80, seg, 0.0))
    return out


def join_segments(segs, lane):
    r = [segs[0]] + [pltpu.roll(segs[q], (80 * q) % 128, axis=1) for q in range(1, 8)]
    return [
        jnp.where(lane < 80, r[0], r[1]),
        jnp.where(lane < 32, r[1], jnp.where(lane < 112, r[2], r[3])),
        jnp.where(lane < 64, r[3], r[4]),
        jnp.where(lane < 16, r[4], jnp.where(lane < 96, r[5], r[6])),
        jnp.where(lane < 48, r[6], r[7]),
    ]


def kernel(
    t_hbm, d_hbm, o_hbm, v_hbm, oooo_hbm, wd_hbm, wx_hbm, out_hbm,
    tf, dbuf, ov, vbuf, ob, wdp, wxb, obuf,
    tcol, ty, tr1, zt, tb, l3, r3o, r5o, zf, zg, fbuf, gbuf, gpart, frecv, grecv,
    xp, prx, pown, xrecv, xpart, xyrecv, msend, mfull,
    lsem, osem, ss, rs,
):
    r = lax.axis_index("row")
    c = lax.axis_index("col")
    k = lax.rem(r, 2)
    x = r // 2
    p1 = r + 1 - 2 * k
    p2 = lax.rem(r + 2, 4)
    p3 = lax.rem(p1 + 2, 4)
    diag = x == c
    off = x != c
    d_p, d_x, d_d, d_y = (c, p1), (c, p2), (c, p3), (1 - c, r)
    other = 2 * (1 - x)
    own = 2 * x

    def rc(src, dst, slot, dev):
        return pltpu.make_async_remote_copy(
            src_ref=src, dst_ref=dst, send_sem=ss.at[slot], recv_sem=rs.at[slot],
            device_id=dev, device_id_type=MESH,
        )

    def wide(n, base=0):
        return pl.ds(pl.multiple_of(base + n * WIDE, 128), WIDE)

    ld_t = pltpu.make_async_copy(t_hbm, tf, lsem.at[0])
    ld_v = pltpu.make_async_copy(v_hbm, vbuf.at[pl.ds(pl.multiple_of(64 * k, 64), 1600)], lsem.at[1])
    ld_wd = pltpu.make_async_copy(wd_hbm, wdp.at[:, pl.ds(0, VIRT)], lsem.at[2])
    ld_wx = pltpu.make_async_copy(wx_hbm, wxb, lsem.at[3])
    ld_o = pltpu.make_async_copy(o_hbm, ov, lsem.at[4])
    ld_d = pltpu.make_async_copy(d_hbm, dbuf, lsem.at[5])
    ld_oooo = pltpu.make_async_copy(oooo_hbm.at[pl.ds(pl.multiple_of(ROWS * r, ROWS), ROWS)], ob, lsem.at[6])
    ld_t.start()

    barrier = pltpu.get_barrier_semaphore()
    for dev in (d_p, d_x, d_d, d_y):
        pl.semaphore_signal(barrier, inc=1, device_id=dev, device_id_type=MESH)
    for ld in (ld_wd, ld_wx, ld_v, ld_o, ld_oooo, ld_d):
        ld.start()
    ld_t.wait()

    @pl.loop(0, 4)
    def _(s):
        rows = pl.ds(pl.multiple_of(16 * s, 16), 16)
        tcol[r, rows] = tf[rows].astype(BF16)

    pl.semaphore_wait(barrier, 4)

    def half(h):
        return pl.ds(32 * h, 32)

    def t_x(h, blk):
        return rc(tcol.at[blk, half(h)], tcol.at[blk, half(h)], T_X + h, d_x)

    def t_y(h):
        return rc(tcol.at[r, half(h)], ty.at[half(h)], T_Y + h, d_y)

    def t_fwd(h, blk):
        return rc(tcol.at[blk, half(h)], tcol.at[blk, half(h)], T_FWD + h, d_p)

    def t_p(blk):
        return rc(tcol.at[blk], tcol.at[blk], T_P, d_p)

    def my_k(core):
        return pl.ds(pl.multiple_of(1536 * core, 128), KPAD)

    def r_p(blk):
        return rc(ty.at[:, my_k(1 - k)], tr1.at[blk], R_P, d_p)

    def r_2(h):
        return rc(tcol.at[p2, half(h), my_k(k)], tr1.at[p2, half(h)], R_2 + h, d_y)

    def r_3(h):
        return rc(tcol.at[p3, half(h), my_k(k)], tr1.at[p3, half(h)], R_3 + h, d_y)

    for h in range(2):
        t_x(h, r).start()
        t_y(h).start()
    t_p(r).start()

    lane64 = lax.broadcasted_iota(jnp.int32, (ROWS, 128), 1)
    vbuf[pl.ds(pl.multiple_of(1600 * (1 - k), 64), 64)] = jnp.zeros((64, COLS), BF16)
    wdp[:, pl.ds(VIRT, 48)] = jnp.zeros((OCC, 48, WIDE), BF16)

    def slabs(ref, col_half):
        @pl.loop(0, NCH)
        def _(g):
            parts = [
                ref[:, pl.ds(pl.multiple_of(g * WIDE + 128 * m, 128), 128)].astype(F32)
                for m in range(5)
            ]
            for q, seg in enumerate(split_segments(parts, lane64)):
                zt[pl.ds(pl.multiple_of((col_half * 40 + g * 8 + q) * ZT, 8), ROWS)] = seg

    slabs(tf, c)

    for h in range(2):
        t_x(h, p2).wait_recv()
        t_fwd(h, p2).start()

        @pl.when(diag)
        def _():
            r_2(h).start()

    for h in range(2):
        t_fwd(h, p3).wait_recv()

        @pl.when(diag)
        def _():
            r_3(h).start()

    for h in range(2):
        t_y(h).wait_recv()

    @pl.when(off)
    def _():
        r_p(r).start()

    slabs(ty, 1 - c)

    for i in range(4):
        @pl.loop(0, OCC)
        def _(kk):
            blk = zt[pl.ds(i * OCC + kk, VIRT, stride=ZT)].astype(BF16)
            tb[i * OCC + kk] = blk
            l3[pl.ds(i * VIRT, VIRT), pl.ds(pl.multiple_of(kk * 128, 128), 128)] = blk

    ld_wd.wait()
    r3o[...] = jnp.dot(l3[...], wdp[...].reshape(OCC * 128, WIDE), preferred_element_type=F32)
    ld_wx.wait()
    rhs = jnp.concatenate([tb[pl.ds(i * OCC, OCC)].reshape(OCC * VIRT, 128) for i in range(4)], axis=1)
    r5o[...] = lax.dot_general(wxb[...], rhs, (((0,), (0,)), ((), ())), preferred_element_type=F32)

    lane80 = lax.broadcasted_iota(jnp.int32, (VIRT, 128), 1)

    @pl.loop(0, 4)
    def _(i):
        rows = pl.ds(pl.multiple_of(i * VIRT, 8), VIRT)
        parts = [r3o[rows, pl.ds(128 * m, 128)] for m in range(5)]
        for j, seg in enumerate(split_segments(parts, lane80)):
            s_ij = seg - r5o[pl.ds(j * VIRT, VIRT), pl.ds(pl.multiple_of(i * 128, 128), 128)]
            zf[pl.ds((j // 4) * 16 + i * 4 + j % 4, VIRT, stride=ZS)] = s_ij
            s_ji = jnp.transpose(jnp.concatenate([s_ij, jnp.zeros((48, 128), F32)], axis=0))
            zg[pl.ds(j * 4 + i, VIRT, stride=ZS)] = s_ji[:VIRT]

    lane32 = lax.broadcasted_iota(jnp.int32, (32, 128), 1)
    for z, flat in ((zg, gbuf), (zf, fbuf)):
        @pl.loop(0, 2 * NCH)
        def _(g):
            segs = [z[pl.ds(pl.multiple_of((g * 8 + q) * ZS, 8), 32)] for q in range(8)]
            for m, tile in enumerate(join_segments(segs, lane32)):
                flat[:, pl.ds(pl.multiple_of(g * WIDE + 128 * m, 128), 128)] = tile

    def g_y(n):
        return rc(gbuf.at[:, wide(n, COLS * (1 - c))], grecv.at[:, wide(n)], G_Y + n, d_y)

    def f_y(n):
        return rc(fbuf.at[:, wide(n, COLS * (1 - c))], frecv.at[:, wide(n)], F_Y + n, d_y)

    def g_p():
        return rc(gbuf.at[pl.ds(pl.multiple_of(16 * (1 - k), 16), 16)], gpart, G_P, d_p)

    @pl.when(off)
    def _():
        for n in range(NCH):
            g_y(n).start()

    @pl.when(off)
    def _():
        @pl.loop(0, NCH)
        def _(n):
            grecv[:, wide(n)] = gbuf[:, wide(n, COLS * c)]

    @pl.when(diag)
    def _():
        g_p().start()
        g_p().wait_recv()
        mine = pl.ds(pl.multiple_of(16 * k, 16), 16)
        theirs = pl.ds(pl.multiple_of(16 * (1 - k), 16), 16)

        @pl.loop(0, 2 * NCH)
        def _(n):
            fbuf[mine, wide(n)] += gbuf[mine, wide(n)]
            fbuf[theirs, wide(n)] += gpart[:, wide(n)]

    for n in range(NCH):
        f_y(n).start()

    @pl.when(diag)
    def _():
        t_p(p1).wait_recv()

        @pl.loop(0, 4)
        def _(b):
            tr1[b] = tcol[b, :, my_k(k)]

    @pl.when(off)
    def _():
        t_p(p1).wait_recv()
        tr1[r] = ty[:, my_k(k)]
        r_p(p1).wait_recv()
        for h in range(2):
            r_2(h).wait_recv()
            r_3(h).wait_recv()

    ld_v.wait()

    def ladder(first, n):
        lhs = tr1[pl.ds(first, 2)].reshape(128, KPAD)
        prod = jnp.dot(lhs, vbuf[:, wide(n)], preferred_element_type=F32)
        xp[pl.ds(first, 2), :, :, :, wide(n)] = prod.reshape(2, 4, 2, 8, WIDE)

    def pair(n, hf, slot):
        return rc(xp.at[p3, :, hf, :, wide(n)], prx.at[:, hf, :, wide(n)], slot + n, d_p)

    def cross(n, hf, slot):
        return rc(xp.at[p2, :, hf, :, wide(n)], xrecv.at[:, hf, :, wide(n)], slot + n, d_x)

    def combine(n, hf, slot_d, slot_x):
        pair(n, hf, slot_d).wait_recv()
        xp[p2, :, hf, :, wide(n)] += prx[:, hf, :, wide(n)]
        cross(n, hf, slot_x).start()

    early, late = 1 - x, x

    @pl.loop(0, NCH)
    def _(n):
        ladder(other, n)
        pair(n, early, E_D).start()

        @pl.when(n > 0)
        def _():
            combine(n - 1, early, E_D, E_X)

    combine(NCH - 1, early, E_D, E_X)

    ld_o.wait()
    xpart[...] = lax.dot_general(
        ov[...], tcol[...].reshape(4 * ROWS, COLS), (((1,), (1,)), ((), ())), preferred_element_type=F32
    )
    x_y = rc(xpart, xyrecv, X_Y, d_y)
    x_y.start()

    def out_pair(n):
        return rc(xp.at[p1, :, :, :, wide(n)], pown.at[:, :, :, wide(n)], O_D + n, d_p)

    @pl.loop(0, NCH)
    def _(n):
        ladder(own, n)
        out_pair(n).start()

    x_y.wait_recv()
    ld_oooo.wait()
    m_rows = (ob[...].astype(F32) + 0.5 * (xpart[...] + xyrecv[...])).astype(BF16)
    for q in range(4):
        msend[q] = m_rows[:, q * ROWS:(q + 1) * ROWS]
    mfull[r] = msend[r]
    m_copies = [
        rc(msend.at[p1], mfull.at[r], M_1, d_p),
        rc(msend.at[p2], mfull.at[r], M_2, d_x),
        rc(msend.at[p3], mfull.at[r], M_3, d_d),
    ]
    for cp in m_copies:
        cp.start()

    row8 = lax.broadcasted_iota(jnp.int32, (8, WIDE), 0)
    here = (row8 // 4) == k

    @pl.loop(0, NCH)
    def _(n):
        @pl.when(diag)
        def _():
            g_y(n).wait_recv()

        for b in range(2):
            for t in range(4):
                g4 = grecv[pl.ds(16 * b + 4 * t, 4), wide(n)]
                g8 = jnp.where(here, jnp.concatenate([g4, g4], axis=0), 0.0)
                xp[other + b, t, late, :, wide(n)] += g8
        pair(n, late, L_D).start()

        @pl.when(n > 0)
        def _():
            combine(n - 1, late, L_D, L_X)

    combine(NCH - 1, late, L_D, L_X)

    for cp in (
        rc(msend.at[p1], mfull.at[p1], M_1, d_p),
        rc(msend.at[p2], mfull.at[p2], M_2, d_x),
        rc(msend.at[p3], mfull.at[p3], M_3, d_d),
    ):
        cp.wait_recv()
    ld_d.wait()

    def put(n):
        return pltpu.make_async_copy(obuf.at[:, wide(n)], out_hbm.at[:, wide(n)], osem.at[n])

    @pl.loop(0, NCH)
    def _(n):
        r2 = lax.dot_general(
            mfull[...].reshape(4 * ROWS, ROWS), tcol[:, :, wide(n)].reshape(4 * ROWS, WIDE),
            (((0,), (0,)), ((), ())), preferred_element_type=F32,
        )
        acc = ov[:, wide(n)].astype(F32) + r2
        out_pair(n).wait_recv()
        f_y(n).wait_recv()
        cross(n, 1 - x, L_X).wait_recv()
        cross(n, x, E_X).wait_recv()
        part = xp[r, :, :, :, wide(n)] + pown[:, :, :, wide(n)] + xrecv[:, :, :, wide(n)]
        acc = acc + part.reshape(ROWS, WIDE)
        obuf[:, wide(n)] = acc
        for i in range(4):
            for ref, hf, base in ((fbuf, c, COLS * c), (frecv, 1 - c, 0)):
                f8 = jnp.concatenate(
                    [ref[pl.ds(4 * i, 4), wide(n, base)], ref[pl.ds(16 + 4 * i, 4), wide(n, base)]], axis=0
                )
                rows = pl.ds(pl.multiple_of(16 * i + 8 * hf, 8), 8)
                obuf[rows, wide(n)] += f8
        obuf[:, wide(n)] = obuf[:, wide(n)] / dbuf[:, wide(n)]
        put(n).start()

    for n in range(NCH):
        put(n).wait()
        f_y(n).wait_send()
        out_pair(n).wait_send()
        pair(n, early, E_D).wait_send()
        pair(n, late, L_D).wait_send()
        cross(n, early, E_X).wait_send()
        cross(n, late, L_X).wait_send()
    for cp in m_copies:
        cp.wait_send()
    x_y.wait_send()
    t_p(r).wait_send()
    for h in range(2):
        t_x(h, r).wait_send()
        t_y(h).wait_send()
        t_fwd(h, p2).wait_send()

    @pl.when(diag)
    def _():
        g_p().wait_send()
        for h in range(2):
            r_2(h).wait_send()
            r_3(h).wait_send()

    @pl.when(off)
    def _():
        r_p(r).wait_send()
        for n in range(NCH):
            g_y(n).wait_send()


def solution(mesh):
    def sweep(t_blk, d_blk, o_blk, v_blk, oooo, wd_blk, wx_blk):
        any_spec = pl.BlockSpec(memory_space=pl.ANY)
        vm = pltpu.VMEM
        return pl.pallas_call(
            kernel,
            out_shape=jax.ShapeDtypeStruct((ROWS, COLS), F32),
            in_specs=[any_spec] * 7,
            out_specs=any_spec,
            scratch_shapes=[
                vm((ROWS, COLS), F32),
                vm((ROWS, COLS), F32),
                vm((ROWS, COLS), BF16),
                vm((KPAD, COLS), BF16),
                vm((ROWS, 256), BF16),
                vm((OCC, 128, WIDE), BF16),
                vm((OCC * VIRT, WIDE), BF16),
                vm((ROWS, COLS), F32),
                vm((4, ROWS, COLS), BF16),
                vm((ROWS, COLS), BF16),
                vm((4, ROWS, KPAD), BF16),
                vm((VIRT * ZT, 128), F32),
                vm((ROWS, VIRT, 128), BF16),
                vm((4 * VIRT, OCC * 128), BF16),
                vm((4 * VIRT, WIDE), F32),
                vm((WIDE, 512), F32),
                vm((VIRT * ZS, 128), F32),
                vm((VIRT * ZS, 128), F32),
                vm((32, 2 * COLS), F32),
                vm((32, 2 * COLS), F32),
                vm((16, 2 * COLS), F32),
                vm((32, COLS), F32),
                vm((32, COLS), F32),
                vm((4, 4, 2, 8, COLS), F32),
                vm((4, 2, 8, COLS), F32),
                vm((4, 2, 8, COLS), F32),
                vm((4, 2, 8, COLS), F32),
                vm((ROWS, 256), F32),
                vm((ROWS, 256), F32),
                vm((4, ROWS, ROWS), BF16),
                vm((4, ROWS, ROWS), BF16),
                pltpu.SemaphoreType.DMA((7,)),
                pltpu.SemaphoreType.DMA((NCH,)),
                pltpu.SemaphoreType.DMA((N_SEM,)),
                pltpu.SemaphoreType.DMA((N_SEM,)),
            ],
            compiler_params=pltpu.CompilerParams(
                collective_id=0, has_side_effects=True, vmem_limit_bytes=60 * 1024 * 1024
            ),
            name="ccd_sweep",
        )(t_blk, d_blk, o_blk, v_blk, oooo, wd_blk.reshape(OCC, VIRT, WIDE), wx_blk)

    amp = P("row", "col")
    wide_spec = P(None, "col")
    return jax.shard_map(
        sweep, mesh=mesh, in_specs=(amp, amp, amp, amp, P(), wide_spec, wide_spec), out_specs=amp, check_vma=False
    )
```

time: 163 us -> 57.6 us (0.35)
  blocking collectives: 65.6 us -> 0 us
  Pallas kernels: 0 us -> 54.9 us
  local copies, waits for them, and re-layouts: 40.5 us -> 2.09 us
  matrix products: 21.7 us -> 0 us
  between operations: 13.3 us -> 0.01 us
  waiting for transfers between devices: 9.35 us -> 0 us
  other arithmetic: 8.54 us -> 0 us
  starting transfers between devices: 3.58 us -> 0 us
    pallas_call x0 -> x1, Pallas kernels: none -> 54.9 us  [sweep(): pl.pallas_call(kernel, out_shape=jax.ShapeDtypeStruct((ROWS, COLS), F32),...]
    all_to_all x3 -> x0, blocking collectives: 52.1 us -> none  [the longest x1 19.7 us: local_sweep(): swap_row = lax.all_to_all(ph_back, 'row', 1, 0, tiled=True)]
    dot_general x5 -> x0, matrix products: 21.7 us -> none  [the longest x1 8.86 us: local_sweep(): jnp.dot(t_ladder, vvvv_blk, preferred_element_type=jnp.float32)]
    all_to_all x10 -> x0, local copies, waits for them, and re-layouts: 15 us -> none  [the longest x3 8.63 us: local_sweep(): swap_both = lax.all_to_all(swap_row, 'col', 3, 2, tiled=True)]
    all_gather x1 -> x0, blocking collectives: 13.5 us -> none  [local_sweep(): t_rows = lax.all_gather(t_half, 'col', axis=1, tiled=True)]
    reshape x4 -> x0, local copies, waits for them, and re-layouts: 12.7 us -> none  [the longest x1 4.07 us: local_sweep(): wd_blk.reshape(n_occ, n_virt, occ_col, n_virt)]
    unnamed x12 -> x1, local copies, waits for them, and re-layouts: 10.7 us -> 2.09 us
    all_to_all x1 -> x0, waiting for transfers between devices: 8.11 us -> none  [local_sweep(): t_ladder = lax.all_to_all(t_rows, 'row', 1, 0, tiled=True)]
  transfers between devices with their start and end apart: 4 -> 0, of which waited for: 2 -> 0; matrix products, arithmetic and copies ran while one was open for 36% -> 0% of each run, Pallas kernels for 0% -> 0%
where the time goes in v1:
time: 57.6 us; the launch traced here: 57 us
  Pallas kernels  54.9 us (95%)
  local copies, waits for them, and re-layouts  2.09 us (4%)
    pallas_call x1, Pallas kernels, sweep(): pl.pallas_call(kernel, out_shape=jax.ShapeDtypeStruct((ROWS, COLS), F32),...  54.9 us
    unnamed x1, local copies, waits for them, and re-layouts  2.09 us

profile of v1, /device:TPU:0, one launch (start us, length us, event | category | flops | bytes accessed | tf_op | source)
XLA Modules:
  0.0 57.0 jit_solution(12661072339008200518)
XLA Ops:
  0.0 54.9 %ccd_sweep.1 = f32[64,3200]{1,0:T(8,128)} custom-call(f32[64,3200]{1,0:T(8,128)} %t_hbm.1, f32[64,3200]{1,0:T(8,128)} %d_hbm.1, bf16[64,3200]{1,0:T(8,128)(2,1)} %o_hbm.1, bf16[1600,3200]{1,0:T(8,128)(2,1)} %v_hbm.1, bf16[256,256]{1,0:T(8,128)(2,1)} %oooo_hbm.1, bf16[16,80,640]{2,1,0:T(8,128)(2,1)} %bitcast.1, bf16[1280,640]{1,0:T(8,128)(2,1)} %wx_hbm.1), custom_call_target="tpu_custom_call" | custom-call | tf_op jit(solution)/shard_map/ccd_sweep/pallas_call | solution.py:414
  54.9 2.1 %copy.9 = f32[64,3200]{1,0:T(8,128)} copy(f32[64,3200]{1,0:T(8,128)} %ccd_sweep.1) | data formatting | bytes 1638400

commit v2 on v1

--- a/solution.py
+++ b/solution.py
@@ -165,12 +165,65 @@
         def _():
             r_3(h).start()
 
+    def ladder(first, n):
+        lhs = tr1[pl.ds(first, 2)].reshape(128, KPAD)
+        prod = jnp.dot(lhs, vbuf[:, wide(n)], preferred_element_type=F32)
+        xp[pl.ds(first, 2), :, :, :, wide(n)] = prod.reshape(2, 4, 2, 8, WIDE)
+
+    def pair(n, hf, slot):
+        return rc(xp.at[p3, :, hf, :, wide(n)], prx.at[:, hf, :, wide(n)], slot + n, d_p)
+
+    def cross(n, hf, slot):
+        return rc(xp.at[p2, :, hf, :, wide(n)], xrecv.at[:, hf, :, wide(n)], slot + n, d_x)
+
+    def combine(n, hf, slot_d, slot_x):
+        pair(n, hf, slot_d).wait_recv()
+        xp[p2, :, hf, :, wide(n)] += prx[:, hf, :, wide(n)]
+        cross(n, hf, slot_x).start()
+
+    early, late = 1 - x, x
+
+    def early_pass():
+        ld_v.wait()
+
+        @pl.loop(0, NCH)
+        def _(n):
+            ladder(other, n)
+            pair(n, early, E_D).start()
+
+            @pl.when(n > 0)
+            def _():
+                combine(n - 1, early, E_D, E_X)
+
+        combine(NCH - 1, early, E_D, E_X)
+
+    @pl.when(diag)
+    def _():
+        t_p(p1).wait_recv()
+
+        @pl.loop(0, 4)
+        def _(b):
+            tr1[b] = tcol[b, :, my_k(k)]
+
+        early_pass()
+
     for h in range(2):
         t_y(h).wait_recv()
 
     @pl.when(off)
     def _():
         r_p(r).start()
+
+    @pl.when(off)
+    def _():
+        t_p(p1).wait_recv()
+
+    ld_o.wait()
+    xpart[...] = lax.dot_general(
+        ov[...], tcol[...].reshape(4 * ROWS, COLS), (((1,), (1,)), ((), ())), preferred_element_type=F32
+    )
+    x_y = rc(xpart, xyrecv, X_Y, d_y)
+    x_y.start()
 
     slabs(ty, 1 - c)
 
@@ -200,12 +253,6 @@
             zg[pl.ds(j * 4 + i, VIRT, stride=ZS)] = s_ji[:VIRT]
 
     lane32 = lax.broadcasted_iota(jnp.int32, (32, 128), 1)
-    for z, flat in ((zg, gbuf), (zf, fbuf)):
-        @pl.loop(0, 2 * NCH)
-        def _(g):
-            segs = [z[pl.ds(pl.multiple_of((g * 8 + q) * ZS, 8), 32)] for q in range(8)]
-            for m, tile in enumerate(join_segments(segs, lane32)):
-                flat[:, pl.ds(pl.multiple_of(g * WIDE + 128 * m, 128), 128)] = tile
 
     def g_y(n):
         return rc(gbuf.at[:, wide(n, COLS * (1 - c))], grecv.at[:, wide(n)], G_Y + n, d_y)
@@ -216,86 +263,67 @@
     def g_p():
         return rc(gbuf.at[pl.ds(pl.multiple_of(16 * (1 - k), 16), 16)], gpart, G_P, d_p)
 
-    @pl.when(off)
-    def _():
-        for n in range(NCH):
+    def flatten(z, g):
+        segs = [z[pl.ds(pl.multiple_of((g * 8 + q) * ZS, 8), 32)] for q in range(8)]
+        return join_segments(segs, lane32)
+
+    @pl.loop(0, NCH)
+    def _(n):
+        for m, tile in enumerate(flatten(zg, n + NCH * (1 - c))):
+            gbuf[:, pl.ds(pl.multiple_of(COLS * (1 - c) + n * WIDE + 128 * m, 128), 128)] = tile
+
+        @pl.when(off)
+        def _():
             g_y(n).start()
 
-    @pl.when(off)
-    def _():
+    @pl.loop(0, NCH)
+    def _(n):
+        tiles = flatten(zg, n + NCH * c)
+
+        @pl.when(diag)
+        def _():
+            for m, tile in enumerate(tiles):
+                gbuf[:, pl.ds(pl.multiple_of(COLS * c + n * WIDE + 128 * m, 128), 128)] = tile
+
+        @pl.when(off)
+        def _():
+            for m, tile in enumerate(tiles):
+                grecv[:, pl.ds(pl.multiple_of(n * WIDE + 128 * m, 128), 128)] = tile
+
+    mine = pl.ds(pl.multiple_of(16 * k, 16), 16)
+    theirs = pl.ds(pl.multiple_of(16 * (1 - k), 16), 16)
+
+    @pl.when(diag)
+    def _():
+        g_p().start()
+        g_p().wait_recv()
+
+    def f_flat(hf, send):
         @pl.loop(0, NCH)
         def _(n):
-            grecv[:, wide(n)] = gbuf[:, wide(n, COLS * c)]
-
-    @pl.when(diag)
-    def _():
-        g_p().start()
-        g_p().wait_recv()
-        mine = pl.ds(pl.multiple_of(16 * k, 16), 16)
-        theirs = pl.ds(pl.multiple_of(16 * (1 - k), 16), 16)
-
-        @pl.loop(0, 2 * NCH)
-        def _(n):
-            fbuf[mine, wide(n)] += gbuf[mine, wide(n)]
-            fbuf[theirs, wide(n)] += gpart[:, wide(n)]
-
-    for n in range(NCH):
-        f_y(n).start()
-
-    @pl.when(diag)
-    def _():
-        t_p(p1).wait_recv()
-
-        @pl.loop(0, 4)
-        def _(b):
-            tr1[b] = tcol[b, :, my_k(k)]
+            for m, tile in enumerate(flatten(zf, n + NCH * hf)):
+                fbuf[:, pl.ds(pl.multiple_of(COLS * hf + n * WIDE + 128 * m, 128), 128)] = tile
+
+            @pl.when(diag)
+            def _():
+                cols = wide(n, COLS * hf)
+                fbuf[mine, cols] += gbuf[mine, cols]
+                fbuf[theirs, cols] += gpart[:, cols]
+
+            if send:
+                f_y(n).start()
+
+    f_flat(1 - c, True)
+    f_flat(c, False)
 
     @pl.when(off)
     def _():
-        t_p(p1).wait_recv()
         tr1[r] = ty[:, my_k(k)]
         r_p(p1).wait_recv()
         for h in range(2):
             r_2(h).wait_recv()
             r_3(h).wait_recv()
-
-    ld_v.wait()
-
-    def ladder(first, n):
-        lhs = tr1[pl.ds(first, 2)].reshape(128, KPAD)
-        prod = jnp.dot(lhs, vbuf[:, wide(n)], preferred_element_type=F32)
-        xp[pl.ds(first, 2), :, :, :, wide(n)] = prod.reshape(2, 4, 2, 8, WIDE)
-
-    def pair(n, hf, slot):
-        return rc(xp.at[p3, :, hf, :, wide(n)], prx.at[:, hf, :, wide(n)], slot + n, d_p)
-
-    def cross(n, hf, slot):
-        return rc(xp.at[p2, :, hf, :, wide(n)], xrecv.at[:, hf, :, wide(n)], slot + n, d_x)
-
-    def combine(n, hf, slot_d, slot_x):
-        pair(n, hf, slot_d).wait_recv()
-        xp[p2, :, hf, :, wide(n)] += prx[:, hf, :, wide(n)]
-        cross(n, hf, slot_x).start()
-
-    early, late = 1 - x, x
-
-    @pl.loop(0, NCH)
-    def _(n):
-        ladder(other, n)
-        pair(n, early, E_D).start()
-
-        @pl.when(n > 0)
-        def _():
-            combine(n - 1, early, E_D, E_X)
-
-    combine(NCH - 1, early, E_D, E_X)
-
-    ld_o.wait()
-    xpart[...] = lax.dot_general(
-        ov[...], tcol[...].reshape(4 * ROWS, COLS), (((1,), (1,)), ((), ())), preferred_element_type=F32
-    )
-    x_y = rc(xpart, xyrecv, X_Y, d_y)
-    x_y.start()
+        early_pass()
 
     def out_pair(n):
         return rc(xp.at[p1, :, :, :, wide(n)], pown.at[:, :, :, wide(n)], O_D + n, d_p)

time: 57.6 us -> 50.1 us (0.87)
  Pallas kernels: 54.9 us -> 47.9 us
    pallas_call x1, Pallas kernels: 54.9 us -> 47.9 us  [sweep(): pl.pallas_call(kernel, out_shape=jax.ShapeDtypeStruct((ROWS, COLS), F32),...]
where the time goes in v2:
time: 50.1 us; the launch traced here: 50 us
  Pallas kernels  47.9 us (96%)
  local copies, waits for them, and re-layouts  2.09 us (4%)
    pallas_call x1, Pallas kernels, sweep(): pl.pallas_call(kernel, out_shape=jax.ShapeDtypeStruct((ROWS, COLS), F32),...  47.9 us
    unnamed x1, local copies, waits for them, and re-layouts  2.09 us

profile of v2, /device:TPU:0, one launch (start us, length us, event | category | flops | bytes accessed | tf_op | source)
XLA Modules:
  0.0 50.0 jit_solution(15582784974135108537)
XLA Ops:
  0.0 47.9 %ccd_sweep.1 = f32[64,3200]{1,0:T(8,128)} custom-call(f32[64,3200]{1,0:T(8,128)} %t_hbm.1, f32[64,3200]{1,0:T(8,128)} %d_hbm.1, bf16[64,3200]{1,0:T(8,128)(2,1)} %o_hbm.1, bf16[1600,3200]{1,0:T(8,128)(2,1)} %v_hbm.1, bf16[256,256]{1,0:T(8,128)(2,1)} %oooo_hbm.1, bf16[16,80,640]{2,1,0:T(8,128)(2,1)} %bitcast.1, bf16[1280,640]{1,0:T(8,128)(2,1)} %wx_hbm.1), custom_call_target="tpu_custom_call" | custom-call | tf_op jit(solution)/shard_map/ccd_sweep/pallas_call | solution.py:442
  47.9 2.1 %copy.9 = f32[64,3200]{1,0:T(8,128)} copy(f32[64,3200]{1,0:T(8,128)} %ccd_sweep.1) | data formatting | bytes 1638400

commit v3 on v1

v3 whole, which is shorter than its diff:
```python
import functools

import jax
import jax.numpy as jnp
from jax import lax
from jax.experimental import pallas as pl
from jax.experimental.pallas import tpu as pltpu
from jax.sharding import PartitionSpec as P

MESH = pl.DeviceIdType.MESH
F32 = jnp.float32
BF16 = jnp.bfloat16

OCC = 16
VIRT = 80
ROWS = 64
COLS = 3200
KPAD = 1664
WIDE = 640
NCH = COLS // WIDE
ZS = 40

T_X, T_Y, T_P, T_FWD, R_P, R_X, R_Y, G_P = 0, 2, 4, 5, 7, 8, 10, 12
E_D, E_X, L_D, L_X, O_D, F_Y, G_Y = 13, 23, 33, 38, 43, 48, 58
X_Y, M_1, M_2, M_3 = 68, 69, 70, 71
N_SEM = 72


def split_segments(parts, lane):
    out = []
    for q in range(8):
        m, s = divmod(80 * q, 128)
        seg = parts[m]
        if s:
            seg = pltpu.roll(seg, 128 - s, axis=1)
            if s + 80 > 128:
                seg = jnp.where(lane < 128 - s, seg, pltpu.roll(parts[m + 1], 128 - s, axis=1))
        out.append(jnp.where(lane < 80, seg, 0.0))
    return out


def join_segments(segs, lane):
    r = [segs[0]] + [pltpu.roll(segs[q], (80 * q) % 128, axis=1) for q in range(1, 8)]
    return [
        jnp.where(lane < 80, r[0], r[1]),
        jnp.where(lane < 32, r[1], jnp.where(lane < 112, r[2], r[3])),
        jnp.where(lane < 64, r[3], r[4]),
        jnp.where(lane < 16, r[4], jnp.where(lane < 96, r[5], r[6])),
        jnp.where(lane < 48, r[6], r[7]),
    ]


def kernel(
    t_hbm, d_hbm, o_hbm, v_hbm, oooo_hbm, wd_hbm, wx_hbm, out_hbm,
    tf, dbuf, ov, vbuf, ob, wdp, wxb, obuf,
    tcol, ty, tr1, zt, tb, l3, r3o, r5o, zf, zg, fbuf, gbuf, gpart, frecv, grecv,
    xp, prx, pown, xrecv, xpart, xyrecv, msend, mfull,
    lsem, osem, ss, rs,
):
    r = lax.axis_index("row")
    c = lax.axis_index("col")
    k = lax.rem(r, 2)
    x = r // 2
    p1 = r + 1 - 2 * k
    p2 = lax.rem(r + 2, 4)
    p3 = lax.rem(p1 + 2, 4)
    diag = x == c
    off = x != c
    d_p, d_x, d_d, d_y, d_z = (c, p1), (c, p2), (c, p3), (1 - c, r), (1 - c, p1)
    other = 2 * (1 - x)
    own = 2 * x

    def rc(src, dst, slot, dev):
        return pltpu.make_async_remote_copy(
            src_ref=src, dst_ref=dst, send_sem=ss.at[slot], recv_sem=rs.at[slot],
            device_id=dev, device_id_type=MESH,
        )

    def wide(n, base=0):
        return pl.ds(pl.multiple_of(base + n * WIDE, 128), WIDE)

    ld_t = pltpu.make_async_copy(t_hbm, tf, lsem.at[0])
    ld_v = pltpu.make_async_copy(v_hbm, vbuf.at[pl.ds(pl.multiple_of(64 * k, 64), 1600)], lsem.at[1])
    ld_wd = pltpu.make_async_copy(wd_hbm, wdp.at[:, pl.ds(0, VIRT)], lsem.at[2])
    ld_wx = pltpu.make_async_copy(wx_hbm, wxb, lsem.at[3])
    ld_o = pltpu.make_async_copy(o_hbm, ov, lsem.at[4])
    ld_d = pltpu.make_async_copy(d_hbm, dbuf, lsem.at[5])
    ld_oooo = pltpu.make_async_copy(oooo_hbm.at[pl.ds(pl.multiple_of(ROWS * r, ROWS), ROWS)], ob, lsem.at[6])
    ld_t.start()

    barrier = pltpu.get_barrier_semaphore()
    for dev in (d_p, d_x, d_d, d_y, d_z):
        pl.semaphore_signal(barrier, inc=1, device_id=dev, device_id_type=MESH)
    for ld in (ld_wd, ld_wx, ld_v, ld_o, ld_oooo, ld_d):
        ld.start()
    ld_t.wait()

    @pl.loop(0, 4)
    def _(s):
        rows = pl.ds(pl.multiple_of(16 * s, 16), 16)
        tcol[r, rows] = tf[rows].astype(BF16)

    pl.semaphore_wait(barrier, 5)

    def half(h):
        return pl.ds(32 * h, 32)

    def t_x(h, blk):
        return rc(tcol.at[blk, half(h)], tcol.at[blk, half(h)], T_X + h, d_x)

    def t_y(h):
        return rc(tcol.at[r, half(h)], ty.at[half(h)], T_Y + h, d_y)

    def t_fwd(h, blk):
        return rc(tcol.at[blk, half(h)], tcol.at[blk, half(h)], T_FWD + h, d_p)

    def t_p(blk):
        return rc(tcol.at[blk], tcol.at[blk], T_P, d_p)

    def my_k(core):
        return pl.ds(pl.multiple_of(1536 * core, 128), KPAD)

    def r_p(blk):
        return rc(ty.at[:, my_k(1 - k)], tr1.at[blk], R_P, d_p)

    def r_x(cross_core):
        core, dev = (1 - k, d_d) if cross_core else (k, d_x)
        return rc(ty.at[half(0), my_k(core)], tr1.at[r, half(0)], R_X + cross_core, dev)

    def r_y(cross_core):
        core, dev = (1 - k, d_z) if cross_core else (k, d_y)
        return rc(tcol.at[p2, half(1), my_k(core)], tr1.at[p2, half(1)], R_Y + cross_core, dev)

    t_x(0, r).start()
    for h in range(2):
        t_y(h).start()

    @pl.when(off)
    def _():
        t_x(1, r).start()

    t_p(r).start()

    lane32 = lax.broadcasted_iota(jnp.int32, (32, 128), 1)
    lane80 = lax.broadcasted_iota(jnp.int32, (VIRT, 128), 1)
    vbuf[pl.ds(pl.multiple_of(1600 * (1 - k), 64), 64)] = jnp.zeros((64, COLS), BF16)
    wdp[:, pl.ds(VIRT, 48)] = jnp.zeros((OCC, 48, WIDE), BF16)

    def slabs(ref, h, col_half):
        @pl.loop(0, NCH)
        def _(g):
            parts = [
                ref[half(h), pl.ds(pl.multiple_of(g * WIDE + 128 * m, 128), 128)].astype(F32)
                for m in range(5)
            ]
            for q, seg in enumerate(split_segments(parts, lane32)):
                zt[h, pl.ds(pl.multiple_of((col_half * 40 + g * 8 + q) * ZS, 8), 32)] = seg

    def s_blocks(h):
        slabs(ty, h, 1 - c)
        for i in range(2):
            @pl.loop(0, OCC)
            def _(kk):
                blk = zt[h, pl.ds(i * OCC + kk, VIRT, stride=ZS)].astype(BF16)
                tb[i * OCC + kk] = blk
                l3[pl.ds(i * VIRT, VIRT), pl.ds(pl.multiple_of(kk * 128, 128), 128)] = blk

        if h == 0:
            ld_wd.wait()
        r3o[...] = jnp.dot(l3[...], wdp[...].reshape(OCC * 128, WIDE), preferred_element_type=F32)
        if h == 0:
            ld_wx.wait()
        rhs = jnp.concatenate([tb[pl.ds(i * OCC, OCC)].reshape(OCC * VIRT, 128) for i in range(2)], axis=1)
        r5o[...] = lax.dot_general(wxb[...], rhs, (((0,), (0,)), ((), ())), preferred_element_type=F32)

        @pl.loop(0, 2)
        def _(i):
            rows = pl.ds(pl.multiple_of(i * VIRT, 8), VIRT)
            parts = [r3o[rows, pl.ds(128 * m, 128)] for m in range(5)]
            for j, seg in enumerate(split_segments(parts, lane80)):
                s_ij = seg - r5o[pl.ds(j * VIRT, VIRT), pl.ds(pl.multiple_of(i * 128, 128), 128)]
                zf[pl.ds((j // 4) * 16 + (2 * h + i) * 4 + j % 4, VIRT, stride=ZS)] = s_ij
                s_ji = jnp.transpose(jnp.concatenate([s_ij, jnp.zeros((48, 128), F32)], axis=0))
                row = jnp.where(diag, j * 4 + 2 * h + i, h * 16 + j * 2 + i)
                zg[pl.ds(row, VIRT, stride=ZS)] = s_ji[:VIRT]

    def tile_at(base, n, m):
        return pl.ds(pl.multiple_of(base + n * WIDE + 128 * m, 128), 128)

    def slab(z, g, q, row, size):
        return z[pl.ds(pl.multiple_of((g * 8 + q) * ZS + row, 8), size)]

    def g_y(n, h):
        rows = pl.ds(16 * h, 16)
        return rc(gbuf.at[rows, wide(n, COLS * (1 - c))], grecv.at[rows, wide(n)], G_Y + NCH * h + n, d_y)

    def f_y(n, h):
        rows = pl.ds(8 * h, 8)
        return rc(fbuf.at[:, rows, wide(n, COLS * (1 - c))], frecv.at[:, rows, wide(n)], F_Y + NCH * h + n, d_y)

    def g_off(h):
        lane16 = lax.broadcasted_iota(jnp.int32, (16, 128), 1)
        rows = pl.ds(16 * h, 16)

        @pl.loop(0, NCH)
        def _(n):
            segs = [slab(zg, n + NCH * (1 - c), q, 16 * h, 16) for q in range(8)]
            for m, tile in enumerate(join_segments(segs, lane16)):
                gbuf[rows, tile_at(COLS * (1 - c), n, m)] = tile
            g_y(n, h).start()

        @pl.loop(0, NCH)
        def _(n):
            segs = [slab(zg, n + NCH * c, q, 16 * h, 16) for q in range(8)]
            for m, tile in enumerate(join_segments(segs, lane16)):
                grecv[rows, tile_at(0, n, m)] = tile

    def f_off(h, send):
        lane8 = lax.broadcasted_iota(jnp.int32, (8, 128), 1)
        rows = pl.ds(8 * h, 8)
        hf = 1 - c if send else c

        @pl.loop(0, NCH)
        def _(n):
            for b in range(2):
                segs = [slab(zf, n + NCH * hf, q, 16 * b + 8 * h, 8) for q in range(8)]
                for m, tile in enumerate(join_segments(segs, lane8)):
                    fbuf[b, rows, tile_at(COLS * hf, n, m)] = tile
            if send:
                f_y(n, h).start()

    def g_p():
        return rc(gbuf.at[pl.ds(pl.multiple_of(16 * (1 - k), 16), 16)], gpart, G_P, d_p)

    def q_diag():
        @pl.loop(0, 2 * NCH)
        def _(n):
            segs = [slab(zg, n, q, 0, 32) for q in range(8)]
            for m, tile in enumerate(join_segments(segs, lane32)):
                gbuf[:, tile_at(0, n, m)] = tile

        g_p().start()
        g_p().wait_recv()
        mine = pl.ds(pl.multiple_of(16 * k, 16), 16)

        for hf in (1 - c, c):
            @pl.loop(0, NCH)
            def _(n):
                segs = [slab(zf, n + NCH * hf, q, 0, 32) for q in range(8)]
                cols = wide(n, COLS * hf)
                for m, tile in enumerate(join_segments(segs, lane32)):
                    at = tile_at(COLS * hf, n, m)
                    fbuf[0, :, at] = tile[:16]
                    fbuf[1, :, at] = tile[16:]
                fbuf[k, :, cols] += gbuf[mine, cols]
                fbuf[1 - k, :, cols] += gpart[:, cols]
                if hf is not c:
                    for h in range(2):
                        f_y(n, h).start()

    for h in range(2):
        slabs(tf, h, c)

    def ladder_own(n):
        lhs = tr1[pl.ds(own, 2)].reshape(128, KPAD)
        prod = jnp.dot(lhs, vbuf[:, wide(n)], preferred_element_type=F32)
        xp[pl.ds(own, 2), :, :, :, wide(n)] = prod.reshape(2, 4, 2, 8, WIDE)

    early, late = 1 - x, x

    def pair_e(n, h):
        ts = pl.ds(2 * h, 2)
        return rc(xp.at[p3, ts, early, :, wide(n)], prx.at[ts, early, :, wide(n)], E_D + NCH * h + n, d_p)

    def cross_e(n, h, hf):
        ts = pl.ds(2 * h, 2)
        return rc(xp.at[p2, ts, hf, :, wide(n)], xrecv.at[ts, hf, :, wide(n)], E_X + NCH * h + n, d_x)

    def pair_l(n):
        return rc(xp.at[p3, :, late, :, wide(n)], prx.at[:, late, :, wide(n)], L_D + n, d_p)

    def cross_l(n, hf):
        return rc(xp.at[p2, :, hf, :, wide(n)], xrecv.at[:, hf, :, wide(n)], L_X + n, d_x)

    def ladder_other(h):
        @pl.loop(0, NCH)
        def _(n):
            lhs = tr1[pl.ds(other, 2), half(h)].reshape(64, KPAD)
            prod = jnp.dot(lhs, vbuf[:, wide(n)], preferred_element_type=F32)
            xp[pl.ds(other, 2), pl.ds(2 * h, 2), :, :, wide(n)] = prod.reshape(2, 2, 2, 8, WIDE)
            pair_e(n, h).start()

    def combine_e(h):
        @pl.loop(0, NCH)
        def _(n):
            ts = pl.ds(2 * h, 2)
            pair_e(n, h).wait_recv()
            xp[p2, ts, early, :, wide(n)] += prx[ts, early, :, wide(n)]
            cross_e(n, h, early).start()

    def combine_l(n):
        pair_l(n).wait_recv()
        xp[p2, :, late, :, wide(n)] += prx[:, late, :, wide(n)]
        cross_l(n, late).start()

    def x_y():
        return rc(xpart, xyrecv, X_Y, d_y)

    def x_part():
        xpart[...] = lax.dot_general(
            ov[...], tcol[...].reshape(4 * ROWS, COLS), (((1,), (1,)), ((), ())), preferred_element_type=F32
        )
        x_y().start()

    def take(h):
        tr1[pl.ds(other, 2), half(h)] = tcol[pl.ds(other, 2), half(h), my_k(k)]

    def send_m():
        x_y().wait_recv()
        m_rows = (ob[...].astype(F32) + 0.5 * (xpart[...] + xyrecv[...])).astype(BF16)
        for q in range(4):
            msend[q] = m_rows[:, q * ROWS:(q + 1) * ROWS]
        mfull[r] = msend[r]
        for cp in m_out():
            cp.start()

    def m_out():
        return (
            rc(msend.at[p1], mfull.at[r], M_1, d_p),
            rc(msend.at[p2], mfull.at[r], M_2, d_x),
            rc(msend.at[p3], mfull.at[r], M_3, d_d),
        )

    def m_in():
        return (
            rc(msend.at[p1], mfull.at[p1], M_1, d_p),
            rc(msend.at[p2], mfull.at[p2], M_2, d_x),
            rc(msend.at[p3], mfull.at[p3], M_3, d_d),
        )

    @pl.when(diag)
    def _():
        t_y(0).wait_recv()
        for q in range(2):
            r_x(q).start()
        t_x(1, r).start()
        t_x(0, p2).wait_recv()
        t_fwd(0, p2).start()
        t_fwd(0, p3).wait_recv()
        take(0)
        ld_v.wait()
        ladder_other(0)
        combine_e(0)
        t_x(1, p2).wait_recv()
        for q in range(2):
            r_y(q).start()
        t_fwd(1, p2).start()
        s_blocks(0)
        t_fwd(1, p3).wait_recv()
        take(1)
        ladder_other(1)
        combine_e(1)
        t_p(p1).wait_recv()
        tr1[r] = tcol[r, :, my_k(k)]
        tr1[p1] = tcol[p1, :, my_k(k)]
        ld_o.wait()
        x_part()
        t_y(1).wait_recv()
        s_blocks(1)
        q_diag()
        ld_oooo.wait()

    @pl.when(off)
    def _():
        t_y(0).wait_recv()
        s_blocks(0)
        g_off(0)
        t_x(0, p2).wait_recv()
        t_fwd(0, p2).start()
        f_off(0, True)
        ld_v.wait()
        for q in range(2):
            r_x(q).wait_recv()
        ladder_other(0)
        combine_e(0)
        t_y(1).wait_recv()
        r_p(r).start()
        tr1[r] = ty[:, my_k(k)]
        s_blocks(1)
        g_off(1)
        t_x(1, p2).wait_recv()
        t_fwd(1, p2).start()
        for q in range(2):
            r_y(q).wait_recv()
        ladder_other(1)
        combine_e(1)
        t_p(p1).wait_recv()
        for h in range(2):
            t_fwd(h, p3).wait_recv()
        ld_o.wait()
        x_part()
        f_off(1, True)
        ld_oooo.wait()
        send_m()
        for h in range(2):
            f_off(h, False)
        r_p(p1).wait_recv()

    def out_pair(n):
        return rc(xp.at[p1, :, :, :, wide(n)], pown.at[:, :, :, wide(n)], O_D + n, d_p)

    row8 = lax.broadcasted_iota(jnp.int32, (8, WIDE), 0)
    here = (row8 // 4) == k

    @pl.loop(0, NCH)
    def _(n):
        ladder_own(n)
        out_pair(n).start()

        @pl.when(diag)
        def _():
            for h in range(2):
                g_y(n, h).wait_recv()

        for b in range(2):
            for t in range(4):
                g2 = [grecv[pl.ds(16 * h + 8 * b + 2 * t, 2), wide(n)] for h in range(2)]
                g8 = jnp.where(here, jnp.concatenate(g2 + g2, axis=0), 0.0)
                xp[other + b, t, late, :, wide(n)] += g8
        pair_l(n).start()

        @pl.when(n > 0)
        def _():
            combine_l(n - 1)

    combine_l(NCH - 1)

    @pl.when(diag)
    def _():
        send_m()

    for cp in m_in():
        cp.wait_recv()
    ld_d.wait()

    def put(n):
        return pltpu.make_async_copy(obuf.at[:, wide(n)], out_hbm.at[:, wide(n)], osem.at[n])

    @pl.loop(0, NCH)
    def _(n):
        r2 = lax.dot_general(
            mfull[...].reshape(4 * ROWS, ROWS), tcol[:, :, wide(n)].reshape(4 * ROWS, WIDE),
            (((0,), (0,)), ((), ())), preferred_element_type=F32,
        )
        acc = ov[:, wide(n)].astype(F32) + r2
        out_pair(n).wait_recv()
        for h in range(2):
            f_y(n, h).wait_recv()
        for h in range(2):
            cross_e(n, h, x).wait_recv()
        cross_l(n, 1 - x).wait_recv()
        part = xp[r, :, :, :, wide(n)] + pown[:, :, :, wide(n)] + xrecv[:, :, :, wide(n)]
        acc = acc + part.reshape(ROWS, WIDE)
        obuf[:, wide(n)] = acc
        for i in range(4):
            for ref, hf, base in ((fbuf, c, COLS * c), (frecv, 1 - c, 0)):
                f8 = jnp.concatenate([ref[b, pl.ds(4 * i, 4), wide(n, base)] for b in range(2)], axis=0)
                rows = pl.ds(pl.multiple_of(16 * i + 8 * hf, 8), 8)
                obuf[rows, wide(n)] += f8
        obuf[:, wide(n)] = obuf[:, wide(n)] / dbuf[:, wide(n)]
        put(n).start()

    for n in range(NCH):
        put(n).wait()
        for h in range(2):
            f_y(n, h).wait_send()
        out_pair(n).wait_send()
        pair_l(n).wait_send()
        cross_l(n, late).wait_send()
        for h in range(2):
            pair_e(n, h).wait_send()
            cross_e(n, h, early).wait_send()
    for cp in m_out():
        cp.wait_send()
    x_y().wait_send()
    t_p(r).wait_send()
    for h in range(2):
        t_x(h, r).wait_send()
        t_y(h).wait_send()
        t_fwd(h, p2).wait_send()

    @pl.when(diag)
    def _():
        g_p().wait_send()
        for q in range(2):
            r_x(q).wait_send()
            r_y(q).wait_send()

    @pl.when(off)
    def _():
        r_p(r).wait_send()
        for n in range(NCH):
            for h in range(2):
                g_y(n, h).wait_send()


def solution(mesh):
    def sweep(t_blk, d_blk, o_blk, v_blk, oooo, wd_blk, wx_blk):
        any_spec = pl.BlockSpec(memory_space=pl.ANY)
        vm = pltpu.VMEM
        return pl.pallas_call(
            kernel,
            out_shape=jax.ShapeDtypeStruct((ROWS, COLS), F32),
            in_specs=[any_spec] * 7,
            out_specs=any_spec,
            scratch_shapes=[
                vm((ROWS, COLS), F32),
                vm((ROWS, COLS), F32),
                vm((ROWS, COLS), BF16),
                vm((KPAD, COLS), BF16),
                vm((ROWS, 256), BF16),
                vm((OCC, 128, WIDE), BF16),
                vm((OCC * VIRT, WIDE), BF16),
                vm((ROWS, COLS), F32),
                vm((4, ROWS, COLS), BF16),
                vm((ROWS, COLS), BF16),
                vm((4, ROWS, KPAD), BF16),
                vm((2, VIRT * ZS, 128), F32),
                vm((32, VIRT, 128), BF16),
                vm((2 * VIRT, OCC * 128), BF16),
                vm((2 * VIRT, WIDE), F32),
                vm((WIDE, 256), F32),
                vm((VIRT * ZS, 128), F32),
                vm((VIRT * ZS, 128), F32),
                vm((2, 16, 2 * COLS), F32),
                vm((32, 2 * COLS), F32),
                vm((16, 2 * COLS), F32),
                vm((2, 16, COLS), F32),
                vm((32, COLS), F32),
                vm((4, 4, 2, 8, COLS), F32),
                vm((4, 2, 8, COLS), F32),
                vm((4, 2, 8, COLS), F32),
                vm((4, 2, 8, COLS), F32),
                vm((ROWS, 256), F32),
                vm((ROWS, 256), F32),
                vm((4, ROWS, ROWS), BF16),
                vm((4, ROWS, ROWS), BF16),
                pltpu.SemaphoreType.DMA((7,)),
                pltpu.SemaphoreType.DMA((NCH,)),
                pltpu.SemaphoreType.DMA((N_SEM,)),
                pltpu.SemaphoreType.DMA((N_SEM,)),
            ],
            compiler_params=pltpu.CompilerParams(
                collective_id=0, has_side_effects=True, vmem_limit_bytes=60 * 1024 * 1024
            ),
            name="ccd_sweep",
        )(t_blk, d_blk, o_blk, v_blk, oooo, wd_blk.reshape(OCC, VIRT, WIDE), wx_blk)

    amp = P("row", "col")
    wide_spec = P(None, "col")
    return jax.shard_map(
        sweep, mesh=mesh, in_specs=(amp, amp, amp, amp, P(), wide_spec, wide_spec), out_specs=amp, check_vma=False
    )
```

time: 57.6 us -> 46.7 us (0.81)
  Pallas kernels: 54.9 us -> 44.5 us
    pallas_call x1, Pallas kernels: 54.9 us -> 44.5 us  [sweep(): pl.pallas_call(kernel, out_shape=jax.ShapeDtypeStruct((ROWS, COLS), F32),...]
where the time goes in v3:
time: 46.7 us; the launch traced here: 46.6 us
  Pallas kernels  44.5 us (95%)
  local copies, waits for them, and re-layouts  2.09 us (4%)
    pallas_call x1, Pallas kernels, sweep(): pl.pallas_call(kernel, out_shape=jax.ShapeDtypeStruct((ROWS, COLS), F32),...  44.5 us
    unnamed x1, local copies, waits for them, and re-layouts  2.09 us

profile of v3, /device:TPU:0, one launch (start us, length us, event | category | flops | bytes accessed | tf_op | source)
XLA Modules:
  0.0 46.6 jit_solution(6945968398058662688)
XLA Ops:
  0.0 44.5 %ccd_sweep.1 = f32[64,3200]{1,0:T(8,128)} custom-call(f32[64,3200]{1,0:T(8,128)} %t_hbm.1, f32[64,3200]{1,0:T(8,128)} %d_hbm.1, bf16[64,3200]{1,0:T(8,128)(2,1)} %o_hbm.1, bf16[1600,3200]{1,0:T(8,128)(2,1)} %v_hbm.1, bf16[256,256]{1,0:T(8,128)(2,1)} %oooo_hbm.1, bf16[16,80,640]{2,1,0:T(8,128)(2,1)} %bitcast.1, bf16[1280,640]{1,0:T(8,128)(2,1)} %wx_hbm.1), custom_call_target="tpu_custom_call" | custom-call | tf_op jit(solution)/shard_map/ccd_sweep/pallas_call | solution.py:511
  44.5 2.1 %copy.9 = f32[64,3200]{1,0:T(8,128)} copy(f32[64,3200]{1,0:T(8,128)} %ccd_sweep.1) | data formatting | bytes 1638400

commit v4 on v3

--- a/solution.py
+++ b/solution.py
@@ -20,10 +20,10 @@
 NCH = COLS // WIDE
 ZS = 40
 
-T_X, T_Y, T_P, T_FWD, R_P, R_X, R_Y, G_P = 0, 2, 4, 5, 7, 8, 10, 12
-E_D, E_X, L_D, L_X, O_D, F_Y, G_Y = 13, 23, 33, 38, 43, 48, 58
-X_Y, M_1, M_2, M_3 = 68, 69, 70, 71
-N_SEM = 72
+T_X, T_Y, T_P, T_FWD, R_P, R_X, R_Y, G_P = 0, 4, 8, 9, 13, 14, 18, 22
+E_D, E_X, L_D, L_X, O_D, F_Y, G_Y = 23, 33, 43, 53, 63, 68, 78
+X_Y, M_1, M_2, M_3 = 88, 89, 90, 91
+N_SEM = 92
 
 
 def split_segments(parts, lane):
@@ -51,11 +51,11 @@
 
 
 def kernel(
-    t_hbm, d_hbm, o_hbm, v_hbm, oooo_hbm, wd_hbm, wx_hbm, out_hbm,
-    tf, dbuf, ov, vbuf, ob, wdp, wxb, obuf,
+    t_hbm, d_hbm, o_hbm, v_hbm, oooo_hbm, wd_hbm, wx_hbm, obuf,
+    tf, dbuf, ov, vbuf, ob, wdp, wxb,
     tcol, ty, tr1, zt, tb, l3, r3o, r5o, zf, zg, fbuf, gbuf, gpart, frecv, grecv,
     xp, prx, pown, xrecv, xpart, xyrecv, msend, mfull,
-    lsem, osem, ss, rs,
+    lsem, ss, rs,
 ):
     r = lax.axis_index("row")
     c = lax.axis_index("col")
@@ -105,14 +105,17 @@
     def half(h):
         return pl.ds(32 * h, 32)
 
-    def t_x(h, blk):
-        return rc(tcol.at[blk, half(h)], tcol.at[blk, half(h)], T_X + h, d_x)
-
-    def t_y(h):
-        return rc(tcol.at[r, half(h)], ty.at[half(h)], T_Y + h, d_y)
-
-    def t_fwd(h, blk):
-        return rc(tcol.at[blk, half(h)], tcol.at[blk, half(h)], T_FWD + h, d_p)
+    def quarter(q):
+        return pl.ds(16 * q, 16)
+
+    def t_x(q, blk):
+        return rc(tcol.at[blk, quarter(q)], tcol.at[blk, quarter(q)], T_X + q, d_x)
+
+    def t_y(q):
+        return rc(tcol.at[r, quarter(q)], ty.at[quarter(q)], T_Y + q, d_y)
+
+    def t_fwd(q, blk):
+        return rc(tcol.at[blk, quarter(q)], tcol.at[blk, quarter(q)], T_FWD + q, d_p)
 
     def t_p(blk):
         return rc(tcol.at[blk], tcol.at[blk], T_P, d_p)
@@ -123,21 +126,24 @@
     def r_p(blk):
         return rc(ty.at[:, my_k(1 - k)], tr1.at[blk], R_P, d_p)
 
-    def r_x(cross_core):
+    def r_x(q, cross_core):
         core, dev = (1 - k, d_d) if cross_core else (k, d_x)
-        return rc(ty.at[half(0), my_k(core)], tr1.at[r, half(0)], R_X + cross_core, dev)
-
-    def r_y(cross_core):
+        return rc(ty.at[quarter(q), my_k(core)], tr1.at[r, quarter(q)], R_X + 2 * q + cross_core, dev)
+
+    def r_y(q, cross_core):
         core, dev = (1 - k, d_z) if cross_core else (k, d_y)
-        return rc(tcol.at[p2, half(1), my_k(core)], tr1.at[p2, half(1)], R_Y + cross_core, dev)
-
-    t_x(0, r).start()
-    for h in range(2):
-        t_y(h).start()
+        return rc(tcol.at[p2, quarter(q), my_k(core)], tr1.at[p2, quarter(q)], R_Y + 2 * (q - 2) + cross_core, dev)
+
+    for q in range(2):
+        t_x(q, r).start()
+        t_y(q).start()
+    for q in range(2, 4):
+        t_y(q).start()
 
     @pl.when(off)
     def _():
-        t_x(1, r).start()
+        for q in range(2, 4):
+            t_x(q, r).start()
 
     t_p(r).start()
 
@@ -240,31 +246,36 @@
                 gbuf[:, tile_at(0, n, m)] = tile
 
         g_p().start()
-        g_p().wait_recv()
-        mine = pl.ds(pl.multiple_of(16 * k, 16), 16)
-
-        for hf in (1 - c, c):
+
+        def flat(hf):
             @pl.loop(0, NCH)
             def _(n):
                 segs = [slab(zf, n + NCH * hf, q, 0, 32) for q in range(8)]
-                cols = wide(n, COLS * hf)
                 for m, tile in enumerate(join_segments(segs, lane32)):
                     at = tile_at(COLS * hf, n, m)
                     fbuf[0, :, at] = tile[:16]
                     fbuf[1, :, at] = tile[16:]
+
+        def add(hf, send):
+            mine = pl.ds(pl.multiple_of(16 * k, 16), 16)
+
+            @pl.loop(0, NCH)
+            def _(n):
+                cols = wide(n, COLS * hf)
                 fbuf[k, :, cols] += gbuf[mine, cols]
                 fbuf[1 - k, :, cols] += gpart[:, cols]
-                if hf is not c:
+                if send:
                     for h in range(2):
                         f_y(n, h).start()
 
+        flat(1 - c)
+        flat(c)
+        g_p().wait_recv()
+        add(1 - c, True)
+        add(c, False)
+
     for h in range(2):
         slabs(tf, h, c)
-
-    def ladder_own(n):
-        lhs = tr1[pl.ds(own, 2)].reshape(128, KPAD)
-        prod = jnp.dot(lhs, vbuf[:, wide(n)], preferred_element_type=F32)
-        xp[pl.ds(own, 2), :, :, :, wide(n)] = prod.reshape(2, 4, 2, 8, WIDE)
 
     early, late = 1 - x, x
 
@@ -276,19 +287,44 @@
         ts = pl.ds(2 * h, 2)
         return rc(xp.at[p2, ts, hf, :, wide(n)], xrecv.at[ts, hf, :, wide(n)], E_X + NCH * h + n, d_x)
 
-    def pair_l(n):
-        return rc(xp.at[p3, :, late, :, wide(n)], prx.at[:, late, :, wide(n)], L_D + n, d_p)
-
-    def cross_l(n, hf):
-        return rc(xp.at[p2, :, hf, :, wide(n)], xrecv.at[:, hf, :, wide(n)], L_X + n, d_x)
-
-    def ladder_other(h):
-        @pl.loop(0, NCH)
-        def _(n):
-            lhs = tr1[pl.ds(other, 2), half(h)].reshape(64, KPAD)
-            prod = jnp.dot(lhs, vbuf[:, wide(n)], preferred_element_type=F32)
-            xp[pl.ds(other, 2), pl.ds(2 * h, 2), :, :, wide(n)] = prod.reshape(2, 2, 2, 8, WIDE)
-            pair_e(n, h).start()
+    def pair_l(n, h):
+        ts = pl.ds(2 * h, 2)
+        return rc(xp.at[p3, ts, late, :, wide(n)], prx.at[ts, late, :, wide(n)], L_D + NCH * h + n, d_p)
+
+    def cross_l(n, h, hf):
+        ts = pl.ds(2 * h, 2)
+        return rc(xp.at[p2, ts, hf, :, wide(n)], xrecv.at[ts, hf, :, wide(n)], L_X + NCH * h + n, d_x)
+
+    def over_columns(step):
+        @pl.loop(0, 2)
+        def _(g):
+            step(pl.ds(pl.multiple_of(g * 2 * WIDE, 128), 2 * WIDE), (2 * g, 2 * g + 1))
+
+        step(pl.ds(4 * WIDE, WIDE), (4,))
+
+    def ladder_0():
+        def step(cols, ns):
+            lhs = tr1[pl.ds(other, 2), half(0)].reshape(64, KPAD)
+            prod = jnp.dot(lhs, vbuf[:, cols], preferred_element_type=F32)
+            xp[pl.ds(other, 2), pl.ds(0, 2), :, :, cols] = prod.reshape(2, 2, 2, 8, -1)
+            for n in ns:
+                pair_e(n, 0).start()
+
+        over_columns(step)
+
+    def ladder_1():
+        def step(cols, ns):
+            lhs = jnp.concatenate(
+                [tr1[pl.ds(other, 2), half(1)].reshape(64, KPAD), tr1[pl.ds(own, 2)].reshape(128, KPAD)], axis=0
+            )
+            prod = jnp.dot(lhs, vbuf[:, cols], preferred_element_type=F32)
+            xp[pl.ds(other, 2), pl.ds(2, 2), :, :, cols] = prod[:64].reshape(2, 2, 2, 8, -1)
+            xp[pl.ds(own, 2), :, :, :, cols] = prod[64:].reshape(2, 4, 2, 8, -1)
+            for n in ns:
+                pair_e(n, 1).start()
+                out_pair(n).start()
+
+        over_columns(step)
 
     def combine_e(h):
         @pl.loop(0, NCH)
@@ -298,10 +334,39 @@
             xp[p2, ts, early, :, wide(n)] += prx[ts, early, :, wide(n)]
             cross_e(n, h, early).start()
 
-    def combine_l(n):
-        pair_l(n).wait_recv()
-        xp[p2, :, late, :, wide(n)] += prx[:, late, :, wide(n)]
-        cross_l(n, late).start()
+    def combine_l(n, h):
+        ts = pl.ds(2 * h, 2)
+        pair_l(n, h).wait_recv()
+        xp[p2, ts, late, :, wide(n)] += prx[ts, late, :, wide(n)]
+        cross_l(n, h, late).start()
+
+    def out_pair(n):
+        return rc(xp.at[p1, :, :, :, wide(n)], pown.at[:, :, :, wide(n)], O_D + n, d_p)
+
+    row8 = lax.broadcasted_iota(jnp.int32, (8, WIDE), 0)
+    here = (row8 // 4) == k
+
+    def late_pass(hs, wait_g):
+        @pl.loop(0, NCH)
+        def _(n):
+            if wait_g:
+                for hh in range(2):
+                    g_y(n, hh).wait_recv()
+            for h in hs:
+                for b in range(2):
+                    for t in (2 * h, 2 * h + 1):
+                        g2 = [grecv[pl.ds(16 * hh + 8 * b + 2 * t, 2), wide(n)] for hh in range(2)]
+                        g8 = jnp.where(here, jnp.concatenate(g2 + g2, axis=0), 0.0)
+                        xp[other + b, t, late, :, wide(n)] += g8
+                pair_l(n, h).start()
+
+            @pl.when(n > 0)
+            def _():
+                for h in hs:
+                    combine_l(n - 1, h)
+
+        for h in hs:
+            combine_l(NCH - 1, h)
 
     def x_y():
         return rc(xpart, xyrecv, X_Y, d_y)
@@ -340,111 +405,94 @@
 
     @pl.when(diag)
     def _():
-        t_y(0).wait_recv()
         for q in range(2):
-            r_x(q).start()
-        t_x(1, r).start()
-        t_x(0, p2).wait_recv()
-        t_fwd(0, p2).start()
-        t_fwd(0, p3).wait_recv()
+            t_y(q).wait_recv()
+            for cc in range(2):
+                r_x(q, cc).start()
+            t_x(q, p2).wait_recv()
+            t_fwd(q, p2).start()
+        for q in range(2, 4):
+            t_x(q, r).start()
+        for q in range(2):
+            t_fwd(q, p3).wait_recv()
         take(0)
         ld_v.wait()
-        ladder_other(0)
+        ladder_0()
         combine_e(0)
-        t_x(1, p2).wait_recv()
-        for q in range(2):
-            r_y(q).start()
-        t_fwd(1, p2).start()
+        t_x(2, p2).wait_recv()
+        t_fwd(2, p2).start()
+        for cc in range(2):
+            r_y(2, cc).start()
         s_blocks(0)
-        t_fwd(1, p3).wait_recv()
-        take(1)
-        ladder_other(1)
-        combine_e(1)
+        t_x(3, p2).wait_recv()
+        t_fwd(3, p2).start()
+        for cc in range(2):
+            r_y(3, cc).start()
         t_p(p1).wait_recv()
         tr1[r] = tcol[r, :, my_k(k)]
         tr1[p1] = tcol[p1, :, my_k(k)]
+        for q in range(2, 4):
+            t_fwd(q, p3).wait_recv()
+        take(1)
+        ladder_1()
+        combine_e(1)
         ld_o.wait()
         x_part()
-        t_y(1).wait_recv()
+        for q in range(2, 4):
+            t_y(q).wait_recv()
         s_blocks(1)
         q_diag()
         ld_oooo.wait()
+        send_m()
+        late_pass((0, 1), True)
 
     @pl.when(off)
     def _():
-        t_y(0).wait_recv()
+        for q in range(2):
+            t_y(q).wait_recv()
         s_blocks(0)
         g_off(0)
-        t_x(0, p2).wait_recv()
-        t_fwd(0, p2).start()
-        f_off(0, True)
-        ld_v.wait()
         for q in range(2):
-            r_x(q).wait_recv()
-        ladder_other(0)
-        combine_e(0)
-        t_y(1).wait_recv()
+            t_x(q, p2).wait_recv()
+            t_fwd(q, p2).start()
+        for q in range(2, 4):
+            t_y(q).wait_recv()
         r_p(r).start()
         tr1[r] = ty[:, my_k(k)]
         s_blocks(1)
         g_off(1)
-        t_x(1, p2).wait_recv()
-        t_fwd(1, p2).start()
+        ld_v.wait()
         for q in range(2):
-            r_y(q).wait_recv()
-        ladder_other(1)
-        combine_e(1)
+            for cc in range(2):
+                r_x(q, cc).wait_recv()
+        ladder_0()
+        combine_e(0)
+        late_pass((0,), False)
+        for q in range(2, 4):
+            t_x(q, p2).wait_recv()
+            t_fwd(q, p2).start()
         t_p(p1).wait_recv()
-        for h in range(2):
-            t_fwd(h, p3).wait_recv()
+        for q in range(4):
+            t_fwd(q, p3).wait_recv()
         ld_o.wait()
         x_part()
-        f_off(1, True)
+        f_off(0, True)
+        for q in range(2, 4):
+            for cc in range(2):
+                r_y(q, cc).wait_recv()
+        r_p(p1).wait_recv()
+        ladder_1()
         ld_oooo.wait()
         send_m()
+        combine_e(1)
+        f_off(1, True)
+        late_pass((1,), False)
         for h in range(2):
             f_off(h, False)
-        r_p(p1).wait_recv()
-
-    def out_pair(n):
-        return rc(xp.at[p1, :, :, :, wide(n)], pown.at[:, :, :, wide(n)], O_D + n, d_p)
-
-    row8 = lax.broadcasted_iota(jnp.int32, (8, WIDE), 0)
-    here = (row8 // 4) == k
-
-    @pl.loop(0, NCH)
-    def _(n):
-        ladder_own(n)
-        out_pair(n).start()
-
-        @pl.when(diag)
-        def _():
-            for h in range(2):
-                g_y(n, h).wait_recv()
-
-        for b in range(2):
-            for t in range(4):
-                g2 = [grecv[pl.ds(16 * h + 8 * b + 2 * t, 2), wide(n)] for h in range(2)]
-                g8 = jnp.where(here, jnp.concatenate(g2 + g2, axis=0), 0.0)
-                xp[other + b, t, late, :, wide(n)] += g8
-        pair_l(n).start()
-
-        @pl.when(n > 0)
-        def _():
-            combine_l(n - 1)
-
-    combine_l(NCH - 1)
-
-    @pl.when(diag)
-    def _():
-        send_m()
 
     for cp in m_in():
         cp.wait_recv()
     ld_d.wait()
-
-    def put(n):
-        return pltpu.make_async_copy(obuf.at[:, wide(n)], out_hbm.at[:, wide(n)], osem.at[n])
 
     @pl.loop(0, NCH)
     def _(n):
@@ -458,7 +506,7 @@
             f_y(n, h).wait_recv()
         for h in range(2):
             cross_e(n, h, x).wait_recv()
-        cross_l(n, 1 - x).wait_recv()
+            cross_l(n, h, 1 - x).wait_recv()
         part = xp[r, :, :, :, wide(n)] + pown[:, :, :, wide(n)] + xrecv[:, :, :, wide(n)]
         acc = acc + part.reshape(ROWS, WIDE)
         obuf[:, wide(n)] = acc
@@ -468,33 +516,31 @@
                 rows = pl.ds(pl.multiple_of(16 * i + 8 * hf, 8), 8)
                 obuf[rows, wide(n)] += f8
         obuf[:, wide(n)] = obuf[:, wide(n)] / dbuf[:, wide(n)]
-        put(n).start()
 
     for n in range(NCH):
-        put(n).wait()
+        out_pair(n).wait_send()
         for h in range(2):
             f_y(n, h).wait_send()
-        out_pair(n).wait_send()
-        pair_l(n).wait_send()
-        cross_l(n, late).wait_send()
-        for h in range(2):
+            pair_l(n, h).wait_send()
+            cross_l(n, h, late).wait_send()
             pair_e(n, h).wait_send()
             cross_e(n, h, early).wait_send()
     for cp in m_out():
         cp.wait_send()
     x_y().wait_send()
     t_p(r).wait_send()
-    for h in range(2):
-        t_x(h, r).wait_send()
-        t_y(h).wait_send()
-        t_fwd(h, p2).wait_send()
+    for q in range(4):
+        t_x(q, r).wait_send()
+        t_y(q).wait_send()
+        t_fwd(q, p2).wait_send()
 
     @pl.when(diag)
     def _():
         g_p().wait_send()
         for q in range(2):
-            r_x(q).wait_send()
-            r_y(q).wait_send()
+            for cc in range(2):
+                r_x(q, cc).wait_send()
+                r_y(q + 2, cc).wait_send()
 
     @pl.when(off)
     def _():
@@ -510,9 +556,9 @@
         vm = pltpu.VMEM
         return pl.pallas_call(
             kernel,
-            out_shape=jax.ShapeDtypeStruct((ROWS, COLS), F32),
+            out_shape=pltpu.VMEM((ROWS, COLS), F32),
             in_specs=[any_spec] * 7,
-            out_specs=any_spec,
+            out_specs=pl.BlockSpec(memory_space=pltpu.VMEM),
             scratch_shapes=[
                 vm((ROWS, COLS), F32),
                 vm((ROWS, COLS), F32),
@@ -521,7 +567,6 @@
                 vm((ROWS, 256), BF16),
                 vm((OCC, 128, WIDE), BF16),
                 vm((OCC * VIRT, WIDE), BF16),
-                vm((ROWS, COLS), F32),
                 vm((4, ROWS, COLS), BF16),
                 vm((ROWS, COLS), BF16),
                 vm((4, ROWS, KPAD), BF16),
@@ -546,12 +591,11 @@
                 vm((4, ROWS, ROWS), BF16),
                 vm((4, ROWS, ROWS), BF16),
                 pltpu.SemaphoreType.DMA((7,)),
-                pltpu.SemaphoreType.DMA((NCH,)),
                 pltpu.SemaphoreType.DMA((N_SEM,)),
                 pltpu.SemaphoreType.DMA((N_SEM,)),
             ],
             compiler_params=pltpu.CompilerParams(
-                collective_id=0, has_side_effects=True, vmem_limit_bytes=60 * 1024 * 1024
+                collective_id=0, has_side_effects=True, vmem_limit_bytes=54 * 1024 * 1024
             ),
             name="ccd_sweep",
         )(t_blk, d_blk, o_blk, v_blk, oooo, wd_blk.reshape(OCC, VIRT, WIDE), wx_blk)

time: 46.7 us -> 43.1 us (0.923)
  Pallas kernels: 44.5 us -> 42.1 us
  local copies, waits for them, and re-layouts: 2.09 us -> 0.89 us
    pallas_call x1, Pallas kernels: 44.5 us -> 42.1 us  [sweep(): pl.pallas_call(kernel, out_shape=pltpu.VMEM((ROWS, COLS), F32), in_specs=...]
    unnamed x1, local copies, waits for them, and re-layouts: 2.09 us -> 0.89 us
where the time goes in v4:
time: 43.1 us; the launch traced here: 43 us
  Pallas kernels  42.1 us (98%)
  local copies, waits for them, and re-layouts  0.89 us (2%)
    pallas_call x1, Pallas kernels, sweep(): pl.pallas_call(kernel, out_shape=pltpu.VMEM((ROWS, COLS), F32), in_specs=...  42.1 us
    unnamed x1, local copies, waits for them, and re-layouts  0.89 us

profile of v4, /device:TPU:0, one launch (start us, length us, event | category | flops | bytes accessed | tf_op | source)
XLA Modules:
  0.0 43.0 jit_solution(10554756877031436636)
XLA Ops:
  0.0 42.1 %ccd_sweep.1 = f32[64,3200]{1,0:T(8,128)S(1)} custom-call(f32[64,3200]{1,0:T(8,128)} %t_hbm.1, f32[64,3200]{1,0:T(8,128)} %d_hbm.1, bf16[64,3200]{1,0:T(8,128)(2,1)} %o_hbm.1, bf16[1600,3200]{1,0:T(8,128)(2,1)} %v_hbm.1, bf16[256,256]{1,0:T(8,128)(2,1)} %oooo_hbm.1, bf16[16,80,640]{2,1,0:T(8,128)(2,1)} %bitcast.1, bf16[1280,640]{1,0:T(8,128)(2,1)} %wx_hbm.1), custom_call_target="tpu_custom_call" | custom-call | tf_op jit(solution)/shard_map/ccd_sweep/pallas_call | solution.py:557
  42.1 0.9 %copy.9 = f32[64,3200]{1,0:T(8,128)} copy(f32[64,3200]{1,0:T(8,128)S(1)} %ccd_sweep.1) | data formatting | bytes 1638400

commit v5 on v4

v5 whole, which is shorter than its diff:
```python
import functools

import jax
import jax.numpy as jnp
from jax import lax
from jax.experimental import pallas as pl
from jax.experimental.pallas import tpu as pltpu
from jax.sharding import PartitionSpec as P

MESH = pl.DeviceIdType.MESH
F32 = jnp.float32
BF16 = jnp.bfloat16

OCC = 16
VIRT = 80
ROWS = 64
COLS = 3200
KPAD = 1664
WIDE = 640
NCH = COLS // WIDE
ZS = 40

T_X, T_Y, T_P, T_FWD, R_P, G_P, R_X, R_Y, G_Y = 0, 4, 7, 8, 10, 10, 11, 13, 11
E_D, L_D, O_D, E_X, L_X, F_Y, X_Y, M_1, M_2, M_3 = 17, 19, 21, 22, 23, 27, 29, 30, 31, 32
N_RECV = 33
S_TX, S_TY, S_TP, S_FWD, S_R, S_PAIR, S_OUT, S_X, S_F, S_G, S_XY, S_M = range(12)
N_SEND = 12


def split_segments(parts, lane):
    out = []
    for q in range(8):
        m, s = divmod(80 * q, 128)
        seg = parts[m]
        if s:
            seg = pltpu.roll(seg, 128 - s, axis=1)
            if s + 80 > 128:
                seg = jnp.where(lane < 128 - s, seg, pltpu.roll(parts[m + 1], 128 - s, axis=1))
        out.append(jnp.where(lane < 80, seg, 0.0))
    return out


def join_segments(segs, lane):
    r = [segs[0]] + [pltpu.roll(segs[q], (80 * q) % 128, axis=1) for q in range(1, 8)]
    return [
        jnp.where(lane < 80, r[0], r[1]),
        jnp.where(lane < 32, r[1], jnp.where(lane < 112, r[2], r[3])),
        jnp.where(lane < 64, r[3], r[4]),
        jnp.where(lane < 16, r[4], jnp.where(lane < 96, r[5], r[6])),
        jnp.where(lane < 48, r[6], r[7]),
    ]


def kernel(
    t_hbm, d_hbm, o_hbm, v_hbm, oooo_hbm, wd_hbm, wx_hbm, obuf,
    tf, dbuf, ov, vbuf, ob, wdp, wxb,
    tcol, ty, tr1, zt, wxs, tb, l3, r3a, r3b, r5a, r5b, zf, zg, gps, gpz, fbuf, gbuf, frecv, grecv,
    xp, prx, pown, xrecv, xpart, xyrecv, msend, mfull,
    lsem, ss, rs,
):
    r = lax.axis_index("row")
    c = lax.axis_index("col")
    k = lax.rem(r, 2)
    x = r // 2
    p1 = r + 1 - 2 * k
    p2 = lax.rem(r + 2, 4)
    p3 = lax.rem(p1 + 2, 4)
    diag = x == c
    off = x != c
    d_p, d_x, d_d, d_y, d_z = (c, p1), (c, p2), (c, p3), (1 - c, r), (1 - c, p1)
    other = 2 * (1 - x)
    own = 2 * x

    def rc(src, dst, leave, arrive, dev):
        return pltpu.make_async_remote_copy(
            src_ref=src, dst_ref=dst, send_sem=ss.at[leave], recv_sem=rs.at[arrive],
            device_id=dev, device_id_type=MESH,
        )

    def wide(n, base=0):
        return pl.ds(pl.multiple_of(base + n * WIDE, 128), WIDE)

    def half(h):
        return pl.ds(32 * h, 32)

    def quarter(q):
        return pl.ds(16 * q, 16)

    def ld_t(q):
        return pltpu.make_async_copy(t_hbm.at[quarter(q)], tf.at[quarter(q)], lsem.at[q])

    ld_v = pltpu.make_async_copy(v_hbm, vbuf.at[pl.ds(pl.multiple_of(64 * k, 64), 1600)], lsem.at[4])
    ld_wd = pltpu.make_async_copy(wd_hbm, wdp.at[:, pl.ds(0, VIRT)], lsem.at[5])
    ld_wx = pltpu.make_async_copy(wx_hbm, wxb, lsem.at[6])
    ld_o = pltpu.make_async_copy(o_hbm, ov, lsem.at[7])
    ld_d = pltpu.make_async_copy(d_hbm, dbuf, lsem.at[8])
    ld_oooo = pltpu.make_async_copy(oooo_hbm.at[pl.ds(pl.multiple_of(ROWS * r, ROWS), ROWS)], ob, lsem.at[9])
    for q in range(4):
        ld_t(q).start()

    barrier = pltpu.get_barrier_semaphore()
    for dev in (d_p, d_x, d_d, d_y, d_z):
        pl.semaphore_signal(barrier, inc=1, device_id=dev, device_id_type=MESH)
    for ld in (ld_wx, ld_wd, ld_v, ld_o, ld_oooo, ld_d):
        ld.start()

    def t_x(q, blk):
        return rc(tcol.at[blk, quarter(q)], tcol.at[blk, quarter(q)], S_TX, T_X + q, d_x)

    def t_y(q):
        return rc(tcol.at[r, quarter(q)], ty.at[quarter(q)], S_TY, T_Y + min(q, 2), d_y)

    def t_y_in():
        return rc(tcol.at[r, half(1)], ty.at[half(1)], S_TY, T_Y + 2, d_y)

    def t_fwd(q):
        return rc(tcol.at[p2, quarter(q)], tcol.at[p2, quarter(q)], S_FWD, T_FWD + q // 2, d_p)

    def t_fwd_in(h):
        return rc(tcol.at[p3, half(h)], tcol.at[p3, half(h)], S_FWD, T_FWD + h, d_p)

    def t_p(blk):
        return rc(tcol.at[blk], tcol.at[blk], S_TP, T_P, d_p)

    def my_k(core):
        return pl.ds(pl.multiple_of(1536 * core, 128), KPAD)

    def r_p(blk):
        return rc(ty.at[:, my_k(1 - k)], tr1.at[blk], S_R, R_P, d_p)

    def r_x(core):
        slot = R_X + lax.rem(k + core, 2)
        return rc(ty.at[quarter(0), my_k(core)], tr1.at[r, quarter(0)], S_R, slot, (c, other + core))

    def r_y(q, core):
        slot = R_Y + 2 * (q > 1) + lax.rem(k + core, 2)
        return rc(tcol.at[p2, quarter(q), my_k(core)], tr1.at[p2, quarter(q)], S_R, slot, (1 - c, own + core))

    def r_y_in(core):
        slot = R_Y + 2 + lax.rem(k + core, 2)
        return rc(tr1.at[p2, half(1)], tr1.at[p2, half(1)], S_R, slot, (1 - c, own + core))

    for q in range(4):
        ld_t(q).wait()
        tcol[r, quarter(q)] = tf[quarter(q)].astype(BF16)
        if q == 0:
            pl.semaphore_wait(barrier, 5)
        if q < 2:
            t_x(q, r).start()
        else:
            pl.when(off)(t_x(q, r).start)
        if q < 3:
            t_y(q).start()
        else:
            pl.when(off)(t_y(q).start)
    t_p(r).start()

    lane32 = lax.broadcasted_iota(jnp.int32, (32, 128), 1)
    lane40 = lax.broadcasted_iota(jnp.int32, (40, 128), 1)
    lane16 = lax.broadcasted_iota(jnp.int32, (16, 128), 1)
    vbuf[pl.ds(pl.multiple_of(1600 * (1 - k), 64), 64)] = jnp.zeros((64, COLS), BF16)
    wdp[:, pl.ds(VIRT, 48)] = jnp.zeros((OCC, 48, WIDE), BF16)

    def slabs(ref, h, col_half):
        @pl.loop(0, NCH)
        def _(g):
            parts = [
                ref[half(h), pl.ds(pl.multiple_of(g * WIDE + 128 * m, 128), 128)].astype(F32)
                for m in range(5)
            ]
            for q, seg in enumerate(split_segments(parts, lane32)):
                zt[h, pl.ds(pl.multiple_of((col_half * 40 + g * 8 + q) * ZS, 8), 32)] = seg

    def regroup(h, vh, l3_rows, tb_at):
        def rows(ik):
            return zt[h, pl.ds(40 * ZS * vh + ik, 40, stride=ZS)]

        @pl.loop(0, OCC)
        def _(kk):
            blk = jnp.concatenate([rows(kk), rows(OCC + kk)], axis=0).astype(BF16)
            l3[l3_rows, pl.ds(pl.multiple_of(kk * 128, 128), 128)] = blk

        for i in range(2):
            @pl.loop(0, OCC // 2)
            def _(k2):
                blk = jnp.concatenate([rows(i * OCC + 2 * k2), rows(i * OCC + 2 * k2 + 1)], axis=0).astype(BF16)
                tb[tb_at + i, pl.ds(pl.multiple_of(k2 * VIRT, 16), VIRT)] = blk

    def r3(rows):
        return jnp.dot(l3[rows], wdp[...].reshape(OCC * 128, WIDE), preferred_element_type=F32)

    def r5(vh, first, count):
        rhs = jnp.concatenate([tb[first + i] for i in range(count)], axis=1)
        return lax.dot_general(wxs[vh], rhs, (((0,), (0,)), ((), ())), preferred_element_type=F32)

    def s_before():
        for h in range(2):
            slabs(tf, h, c)
        ld_wx.wait()

        @pl.loop(0, OCC // 2)
        def _(k2):
            w = [wxb[2 * k2 + e].astype(F32) for e in range(2)]
            at = pl.ds(pl.multiple_of(k2 * VIRT, 16), VIRT)
            for vh in range(2):
                part = [w[e][40 * vh:40 * vh + 40] for e in range(2)]
                wxs[vh, at] = jnp.concatenate(part, axis=0).astype(BF16)

        for h in range(2):
            regroup(h, c, pl.ds(VIRT * h, VIRT), 2 * h)
        ld_wd.wait()
        r3a[...] = r3(pl.ds(0, 2 * VIRT))
        r5a[...] = r5(c, 0, 4)

    def s_prep(h):
        slabs(ty, h, 1 - c)
        regroup(h, 1 - c, pl.ds(0, VIRT), 0)

    def s_blocks(h):
        r3b[...] = r3(pl.ds(0, VIRT))
        r5b[...] = r5a[:, 256 * h:256 * h + 256] + r5(1 - c, 0, 2)

        @pl.loop(0, 2)
        def _(i):
            rows_a = pl.ds(pl.multiple_of(VIRT * h + 40 * i, 8), 40)
            rows_b = pl.ds(pl.multiple_of(40 * i, 8), 40)
            seg_a = split_segments([r3a[rows_a, pl.ds(128 * m, 128)] for m in range(5)], lane40)
            seg_b = split_segments([r3b[rows_b, pl.ds(128 * m, 128)] for m in range(5)], lane40)
            lanes = pl.ds(pl.multiple_of(i * 128, 128), 128)
            for j in range(8):
                s_a = seg_a[j] - r5b[pl.ds(pl.multiple_of(j * VIRT + 40 * c, 8), 40), lanes]
                s_b = seg_b[j] - r5b[pl.ds(pl.multiple_of(j * VIRT + 40 * (1 - c), 8), 40), lanes]
                row = (j // 4) * 16 + (2 * h + i) * 4 + j % 4
                zf[pl.ds(40 * ZS * c + row, 40, stride=ZS)] = s_a
                zf[pl.ds(40 * ZS * (1 - c) + row, 40, stride=ZS)] = s_b
                both = [jnp.where(c == 0, s_a, s_b), jnp.where(c == 0, s_b, s_a), jnp.zeros((48, 128), F32)]
                row = jnp.where(diag, j * 4 + 2 * h + i, h * 16 + j * 2 + i)
                zg[pl.ds(row, VIRT, stride=ZS)] = jnp.transpose(jnp.concatenate(both, axis=0))[:VIRT]

    def tile_at(base, n, m):
        return pl.ds(pl.multiple_of(base + n * WIDE + 128 * m, 128), 128)

    def slab(z, g, q, row, size):
        return z[pl.ds(pl.multiple_of((g * 8 + q) * ZS + row, 8), size)]

    def g_y(n, h):
        rows = pl.ds(16 * h, 16)
        return rc(gbuf.at[rows, wide(n)], grecv.at[rows, wide(n)], S_G, G_Y + h, d_y)

    def g_y_in(h):
        return rc(gbuf.at[pl.ds(16 * h, 16)], grecv.at[pl.ds(16 * h, 16)], S_G, G_Y + h, d_y)

    def f_y_in(h):
        rows = pl.ds(8 * h, 8)
        return rc(frecv.at[:, rows], frecv.at[:, rows], S_F, F_Y + h, d_y)

    def f_y(n, h):
        rows = pl.ds(8 * h, 8)
        return rc(fbuf.at[:, rows, wide(n, COLS * (1 - c))], frecv.at[:, rows, wide(n)], S_F, F_Y + h, d_y)

    def g_off(h):
        rows = pl.ds(16 * h, 16)

        @pl.loop(0, NCH)
        def _(n):
            segs = [slab(zg, n + NCH * (1 - c), q, 16 * h, 16) for q in range(8)]
            for m, tile in enumerate(join_segments(segs, lane16)):
                gbuf[rows, tile_at(0, n, m)] = tile
            g_y(n, h).start()

        @pl.loop(0, NCH)
        def _(n):
            segs = [slab(zg, n + NCH * c, q, 16 * h, 16) for q in range(8)]
            for m, tile in enumerate(join_segments(segs, lane16)):
                grecv[rows, tile_at(0, n, m)] = tile

    def f_off(h, send):
        lane8 = lax.broadcasted_iota(jnp.int32, (8, 128), 1)
        rows = pl.ds(8 * h, 8)
        hf = 1 - c if send else c

        @pl.loop(0, NCH)
        def _(n):
            for b in range(2):
                segs = [slab(zf, n + NCH * hf, q, 16 * b + 8 * h, 8) for q in range(8)]
                for m, tile in enumerate(join_segments(segs, lane8)):
                    fbuf[b, rows, tile_at(COLS * hf, n, m)] = tile
            if send:
                f_y(n, h).start()

    def g_p():
        return rc(gps, gpz, S_G, G_P, d_p)

    def give_g():
        @pl.loop(0, VIRT, unroll=8)
        def _(v):
            gps[v] = zg[pl.ds(pl.multiple_of(v * ZS + 16 * (1 - k), 8), 16)]

        g_p().start()

    def q_diag():
        g_p().wait_recv()

        def flat(hf, send):
            @pl.loop(0, NCH)
            def _(n):
                for b, mine in ((k, True), (1 - k, False)):
                    row = pl.multiple_of(16 * b, 16)
                    segs = []
                    for q in range(8):
                        g = n + NCH * hf
                        extra = slab(zg, g, q, row, 16) if mine else gpz[g * 8 + q]
                        segs.append(slab(zf, g, q, row, 16) + extra)
                    for m, tile in enumerate(join_segments(segs, lane16)):
                        fbuf[b, :, tile_at(COLS * hf, n, m)] = tile
                if send:
                    for h in range(2):
                        f_y(n, h).start()

        flat(1 - c, True)
        flat(c, False)

    s_before()

    early, late = 1 - x, x

    def pair(hf, h, cols, slot):
        ts = pl.ds(2 * h, 2)
        return rc(xp.at[p3, ts, hf, :, cols], prx.at[ts, hf, :, cols], S_PAIR, slot, d_p)

    def pair_e(n, h):
        return pair(early, h, wide(n), E_D + h)

    def pair_l(n, h):
        return pair(late, h, wide(n), L_D + h)

    def cross(hf, h, cols, slot):
        ts = pl.ds(2 * h, 2)
        return rc(xp.at[p2, ts, hf, :, cols], xrecv.at[ts, hf, :, cols], S_X, slot, d_x)

    def combine(hf, h, first, last, slot):
        @pl.loop(first, last)
        def _(n):
            ts = pl.ds(2 * h, 2)
            xp[p2, ts, hf, :, wide(n)] += prx[ts, hf, :, wide(n)]
            cross(hf, h, wide(n), slot(n)).start()

    def over_columns(step):
        @pl.loop(0, 2)
        def _(g):
            step(pl.ds(pl.multiple_of(g * 2 * WIDE, 128), 2 * WIDE), (2 * g, 2 * g + 1))

        step(pl.ds(4 * WIDE, WIDE), (4,))

    def ladder_0():
        def step(cols, ns):
            lhs = tr1[pl.ds(other, 2), half(0)].reshape(64, KPAD)
            prod = jnp.dot(lhs, vbuf[:, cols], preferred_element_type=F32)
            xp[pl.ds(other, 2), pl.ds(0, 2), :, :, cols] = prod.reshape(2, 2, 2, 8, -1)
            for n in ns:
                pair_e(n, 0).start()

        over_columns(step)

    def ladder_1():
        def step(cols, ns):
            lhs = jnp.concatenate(
                [tr1[pl.ds(other, 2), half(1)].reshape(64, KPAD), tr1[pl.ds(own, 2)].reshape(128, KPAD)], axis=0
            )
            prod = jnp.dot(lhs, vbuf[:, cols], preferred_element_type=F32)
            xp[pl.ds(other, 2), pl.ds(2, 2), :, :, cols] = prod[:64].reshape(2, 2, 2, 8, -1)
            xp[pl.ds(own, 2), :, :, :, cols] = prod[64:].reshape(2, 4, 2, 8, -1)
            for n in ns:
                pair_e(n, 1).start()
                out_pair(n).start()

        over_columns(step)

    def combine_e(h):
        pair(early, h, pl.ds(0, COLS), E_D + h).wait_recv()
        combine(early, h, 0, NCH, lambda n: E_X)

    def combine_l(h, first=0, last=NCH):
        if first == 0:
            pair(late, h, pl.ds(0, COLS), L_D + h).wait_recv()
        combine(late, h, first, last, lambda n: L_X + 1 + n // 2 if h else L_X)

    def out_pair(n):
        return rc(xp.at[p1, :, :, :, wide(n)], pown.at[:, :, :, wide(n)], S_OUT, O_D, d_p)

    row8 = lax.broadcasted_iota(jnp.int32, (8, WIDE), 0)
    here = (row8 // 4) == k

    def late_add(hs, wait_g):
        if wait_g:
            for hh in range(2):
                g_y_in(hh).wait_recv()

        @pl.loop(0, NCH)
        def _(n):
            for h in hs:
                for b in range(2):
                    for t in (2 * h, 2 * h + 1):
                        g2 = [grecv[pl.ds(16 * hh + 8 * b + 2 * t, 2), wide(n)] for hh in range(2)]
                        g8 = jnp.where(here, jnp.concatenate(g2 + g2, axis=0), 0.0)
                        xp[other + b, t, late, :, wide(n)] += g8
                pair_l(n, h).start()

    def x_y():
        return rc(xpart, xyrecv, S_XY, X_Y, d_y)

    def x_part():
        xpart[...] = lax.dot_general(
            ov[...], tcol[...].reshape(4 * ROWS, COLS), (((1,), (1,)), ((), ())), preferred_element_type=F32
        )
        x_y().start()

    def take(h):
        tr1[pl.ds(other, 2), half(h)] = tcol[pl.ds(other, 2), half(h), my_k(k)]

    def send_m():
        x_y().wait_recv()
        m_rows = (ob[...].astype(F32) + 0.5 * (xpart[...] + xyrecv[...])).astype(BF16)
        for q in range(4):
            msend[q] = m_rows[:, q * ROWS:(q + 1) * ROWS]
        mfull[r] = msend[r]
        for cp in m_out():
            cp.start()

    def m_out():
        return (
            rc(msend.at[p1], mfull.at[r], S_M, M_1, d_p),
            rc(msend.at[p2], mfull.at[r], S_M, M_2, d_x),
            rc(msend.at[p3], mfull.at[r], S_M, M_3, d_d),
        )

    def m_in():
        return (
            rc(msend.at[p1], mfull.at[p1], S_M, M_1, d_p),
            rc(msend.at[p2], mfull.at[p2], S_M, M_2, d_x),
            rc(msend.at[p3], mfull.at[p3], S_M, M_3, d_d),
        )

    @pl.when(diag)
    def _():
        t_y(0).wait_recv()
        for cc in (1, 0):
            r_x(cc).start()
        for q in range(2, 4):
            t_x(q, r).start()
        t_x(0, p2).wait_recv()
        t_fwd(0).start()
        t_x(1, p2).wait_recv()
        t_fwd(1).start()
        for cc in (1, 0):
            r_y(1, cc).start()
        t_y(3).start()
        t_fwd_in(0).wait_recv()
        take(0)
        ld_v.wait()
        ladder_0()
        t_y(1).wait_recv()
        s_prep(0)
        for q in range(2, 4):
            t_x(q, p2).wait_recv()
            t_fwd(q).start()
            for cc in (1, 0):
                r_y(q, cc).start()
        combine_e(0)
        s_blocks(0)
        t_p(p1).wait_recv()
        tr1[r] = tcol[r, :, my_k(k)]
        tr1[p1] = tcol[p1, :, my_k(k)]
        t_fwd_in(1).wait_recv()
        take(1)
        ladder_1()
        ld_o.wait()
        x_part()
        combine_e(1)
        t_y_in().wait_recv()
        s_prep(1)
        s_blocks(1)
        give_g()
        q_diag()
        late_add((0, 1), True)
        combine_l(0)
        combine_l(1, 0, 3)
        ld_oooo.wait()
        send_m()
        combine_l(1, 3)

    @pl.when(off)
    def _():
        for q in range(2):
            t_y(q).wait_recv()
        s_prep(0)
        s_blocks(0)
        g_off(0)
        for q in range(2):
            t_x(q, p2).wait_recv()
            t_fwd(q).start()
        ld_v.wait()
        for cc in (1, 0):
            r_x(cc).wait_recv()
            r_y(1, cc).wait_recv()
        ladder_0()
        t_y_in().wait_recv()
        r_p(r).start()
        tr1[r] = ty[:, my_k(k)]
        s_prep(1)
        for q in range(2, 4):
            t_x(q, p2).wait_recv()
            t_fwd(q).start()
        combine_e(0)
        s_blocks(1)
        g_off(1)
        late_add((0,), False)
        t_p(p1).wait_recv()
        for h in range(2):
            t_fwd_in(h).wait_recv()
        ld_o.wait()
        x_part()
        combine_l(0)
        f_off(0, True)
        for cc in (1, 0):
            r_y_in(cc).wait_recv()
        r_p(p1).wait_recv()
        ladder_1()
        late_add((1,), False)
        ld_oooo.wait()
        send_m()
        combine_e(1)
        f_off(1, True)
        combine_l(1)
        for h in range(2):
            f_off(h, False)

    for cp in m_in():
        cp.wait_recv()
    ld_d.wait()
    rc(xp.at[p1], pown, S_OUT, O_D, d_p).wait_recv()
    for h in range(2):
        f_y_in(h).wait_recv()
    rc(xp.at[p2, :, x], xrecv.at[:, x], S_X, E_X, d_x).wait_recv()
    cross(1 - x, 0, pl.ds(0, COLS), L_X).wait_recv()

    def finish(cols, ns):
        cross(1 - x, 1, cols, L_X + 1 + ns[0] // 2).wait_recv()
        width = len(ns) * WIDE
        r2 = lax.dot_general(
            mfull[...].reshape(4 * ROWS, ROWS), tcol[:, :, cols].reshape(4 * ROWS, width),
            (((0,), (0,)), ((), ())), preferred_element_type=F32,
        )
        part = xp[r, :, :, :, cols] + pown[:, :, :, cols] + xrecv[:, :, :, cols]
        obuf[:, cols] = ov[:, cols].astype(F32) + r2 + part.reshape(ROWS, width)
        mine = pl.ds(pl.multiple_of(COLS * c + ns[0] * WIDE, 128), width)
        for i in range(4):
            for ref, hf, at in ((fbuf, c, mine), (frecv, 1 - c, cols)):
                f8 = jnp.concatenate([ref[b, pl.ds(4 * i, 4), at] for b in range(2)], axis=0)
                rows = pl.ds(pl.multiple_of(16 * i + 8 * hf, 8), 8)
                obuf[rows, cols] += f8
        obuf[:, cols] = obuf[:, cols] / dbuf[:, cols]

    over_columns(finish)

    rc(tcol.at[r], tcol.at[r], S_TX, T_X, d_x).wait_send()
    rc(tcol.at[r], ty, S_TY, T_Y, d_y).wait_send()
    rc(tcol.at[p2], tcol.at[p2], S_FWD, T_FWD, d_p).wait_send()
    t_p(r).wait_send()
    rc(xp.at[p3], prx, S_PAIR, E_D, d_p).wait_send()
    rc(xp.at[p1], pown, S_OUT, O_D, d_p).wait_send()
    rc(xp.at[p2], xrecv, S_X, E_X, d_x).wait_send()
    rc(frecv, frecv, S_F, F_Y, d_y).wait_send()
    x_y().wait_send()
    rc(msend.at[pl.ds(0, 3)], mfull.at[pl.ds(0, 3)], S_M, M_1, d_p).wait_send()

    @pl.when(diag)
    def _():
        g_p().wait_send()
        rc(tr1.at[pl.ds(0, 2)], tr1.at[pl.ds(0, 2)], S_R, R_Y, d_y).wait_send()

    @pl.when(off)
    def _():
        r_p(r).wait_send()
        rc(gbuf, grecv, S_G, G_Y, d_y).wait_send()


def solution(mesh):
    def sweep(t_blk, d_blk, o_blk, v_blk, oooo, wd_blk, wx_blk):
        any_spec = pl.BlockSpec(memory_space=pl.ANY)
        vm = pltpu.VMEM
        return pl.pallas_call(
            kernel,
            out_shape=pltpu.VMEM((ROWS, COLS), F32),
            in_specs=[any_spec] * 7,
            out_specs=pl.BlockSpec(memory_space=pltpu.VMEM),
            scratch_shapes=[
                vm((ROWS, COLS), F32),
                vm((ROWS, COLS), F32),
                vm((ROWS, COLS), BF16),
                vm((KPAD, COLS), BF16),
                vm((ROWS, 256), BF16),
                vm((OCC, 128, WIDE), BF16),
                vm((OCC, VIRT, WIDE), BF16),
                vm((4, ROWS, COLS), BF16),
                vm((ROWS, COLS), BF16),
                vm((4, ROWS, KPAD), BF16),
                vm((2, VIRT * ZS, 128), F32),
                vm((2, WIDE, WIDE), BF16),
                vm((4, WIDE, 128), BF16),
                vm((2 * VIRT, OCC * 128), BF16),
                vm((2 * VIRT, WIDE), F32),
                vm((VIRT, WIDE), F32),
                vm((WIDE, 512), F32),
                vm((WIDE, 256), F32),
                vm((VIRT * ZS, 128), F32),
                vm((VIRT * ZS, 128), F32),
                vm((VIRT, 16, 128), F32),
                vm((VIRT, 16, 128), F32),
                vm((2, 16, 2 * COLS), F32),
                vm((32, COLS), F32),
                vm((2, 16, COLS), F32),
                vm((32, COLS), F32),
                vm((4, 4, 2, 8, COLS), F32),
                vm((4, 2, 8, COLS), F32),
                vm((4, 2, 8, COLS), F32),
                vm((4, 2, 8, COLS), F32),
                vm((ROWS, 256), F32),
                vm((ROWS, 256), F32),
                vm((4, ROWS, ROWS), BF16),
                vm((4, ROWS, ROWS), BF16),
                pltpu.SemaphoreType.DMA((10,)),
                pltpu.SemaphoreType.DMA((N_SEND,)),
                pltpu.SemaphoreType.DMA((N_RECV,)),
            ],
            compiler_params=pltpu.CompilerParams(
                collective_id=0, has_side_effects=True, vmem_limit_bytes=54 * 1024 * 1024
            ),
            name="ccd_sweep",
        )(t_blk, d_blk, o_blk, v_blk, oooo, wd_blk.reshape(OCC, VIRT, WIDE), wx_blk.reshape(OCC, VIRT, WIDE))

    amp = P("row", "col")
    wide_spec = P(None, "col")
    return jax.shard_map(
        sweep, mesh=mesh, in_specs=(amp, amp, amp, amp, P(), wide_spec, wide_spec), out_specs=amp, check_vma=False
    )
```

time: 43.1 us -> 40.5 us (0.940)
  Pallas kernels: 42.1 us -> 39.5 us
    pallas_call x1, Pallas kernels: 42.1 us -> 39.5 us  [sweep(): pl.pallas_call(kernel, out_shape=pltpu.VMEM((ROWS, COLS), F32), in_specs=...]
where the time goes in v5:
time: 40.5 us; the launch traced here: 40.4 us
  Pallas kernels  39.5 us (98%)
  local copies, waits for them, and re-layouts  0.89 us (2%)
    pallas_call x1, Pallas kernels, sweep(): pl.pallas_call(kernel, out_shape=pltpu.VMEM((ROWS, COLS), F32), in_specs=...  39.5 us
    unnamed x1, local copies, waits for them, and re-layouts  0.89 us

profile of v5, /device:TPU:0, one launch (start us, length us, event | category | flops | bytes accessed | tf_op | source)
XLA Modules:
  0.0 40.4 jit_solution(16033615428375916959)
XLA Ops:
  0.0 39.5 %ccd_sweep.1 = f32[64,3200]{1,0:T(8,128)S(1)} custom-call(f32[64,3200]{1,0:T(8,128)} %t_hbm.1, f32[64,3200]{1,0:T(8,128)} %d_hbm.1, bf16[64,3200]{1,0:T(8,128)(2,1)} %o_hbm.1, bf16[1600,3200]{1,0:T(8,128)(2,1)} %v_hbm.1, bf16[256,256]{1,0:T(8,128)(2,1)} %oooo_hbm.1, bf16[16,80,640]{2,1,0:T(8,128)(2,1)} %bitcast.2, bf16[16,80,640]{2,1,0:T(8,128)(2,1)} %bitcast.3), custom_call_target="tpu_custom_call" | custom-call | tf_op jit(solution)/shard_map/ccd_sweep/pallas_call | solution.py:592
  39.5 0.9 %copy.9 = f32[64,3200]{1,0:T(8,128)} copy(f32[64,3200]{1,0:T(8,128)S(1)} %ccd_sweep.1) | data formatting | bytes 1638400

commit v6 on v5

--- a/solution.py
+++ b/solution.py
@@ -16,13 +16,16 @@
 ROWS = 64
 COLS = 3200
 KPAD = 1664
+LANE = 128
+HALF_V = VIRT // 2
+BOTH = range(2)
 WIDE = 640
 NCH = COLS // WIDE
 ZS = 40
 
 T_X, T_Y, T_P, T_FWD, R_P, G_P, R_X, R_Y, G_Y = 0, 4, 7, 8, 10, 10, 11, 13, 11
-E_D, L_D, O_D, E_X, L_X, F_Y, X_Y, M_1, M_2, M_3 = 17, 19, 21, 22, 23, 27, 29, 30, 31, 32
-N_RECV = 33
+E_D, L_D, O_D, E_X, L_X, F_Y, X_Y, M_1, M_2, M_3 = 17, 23, 25, 26, 27, 31, 33, 34, 35, 36
+N_RECV = 37
 S_TX, S_TY, S_TP, S_FWD, S_R, S_PAIR, S_OUT, S_X, S_F, S_G, S_XY, S_M = range(12)
 N_SEND = 12
 
@@ -30,18 +33,18 @@
 def split_segments(parts, lane):
     out = []
     for q in range(8):
-        m, s = divmod(80 * q, 128)
+        m, s = divmod(80 * q, LANE)
         seg = parts[m]
         if s:
-            seg = pltpu.roll(seg, 128 - s, axis=1)
-            if s + 80 > 128:
-                seg = jnp.where(lane < 128 - s, seg, pltpu.roll(parts[m + 1], 128 - s, axis=1))
+            seg = pltpu.roll(seg, LANE - s, axis=1)
+            if s + 80 > LANE:
+                seg = jnp.where(lane < LANE - s, seg, pltpu.roll(parts[m + 1], LANE - s, axis=1))
         out.append(jnp.where(lane < 80, seg, 0.0))
     return out
 
 
 def join_segments(segs, lane):
-    r = [segs[0]] + [pltpu.roll(segs[q], (80 * q) % 128, axis=1) for q in range(1, 8)]
+    r = [segs[0]] + [pltpu.roll(segs[q], (80 * q) % LANE, axis=1) for q in range(1, 8)]
     return [
         jnp.where(lane < 80, r[0], r[1]),
         jnp.where(lane < 32, r[1], jnp.where(lane < 112, r[2], r[3])),
@@ -78,7 +81,7 @@
         )
 
     def wide(n, base=0):
-        return pl.ds(pl.multiple_of(base + n * WIDE, 128), WIDE)
+        return pl.ds(pl.multiple_of(base + n * WIDE, LANE), WIDE)
 
     def half(h):
         return pl.ds(32 * h, 32)
@@ -123,17 +126,17 @@
         return rc(tcol.at[blk], tcol.at[blk], S_TP, T_P, d_p)
 
     def my_k(core):
-        return pl.ds(pl.multiple_of(1536 * core, 128), KPAD)
+        return pl.ds(pl.multiple_of(1536 * core, LANE), KPAD)
 
     def r_p(blk):
         return rc(ty.at[:, my_k(1 - k)], tr1.at[blk], S_R, R_P, d_p)
 
-    def r_x(core):
-        slot = R_X + lax.rem(k + core, 2)
-        return rc(ty.at[quarter(0), my_k(core)], tr1.at[r, quarter(0)], S_R, slot, (c, other + core))
+    def r_x(q, core):
+        slot = R_Y if q else R_X + lax.rem(k + core, 2)
+        return rc(ty.at[quarter(q), my_k(core)], tr1.at[r, quarter(q)], S_R, slot, (c, other + core))
 
     def r_y(q, core):
-        slot = R_Y + 2 * (q > 1) + lax.rem(k + core, 2)
+        slot = R_Y + 1 if q == 1 else R_Y + 2 + lax.rem(k + core, 2)
         return rc(tcol.at[p2, quarter(q), my_k(core)], tr1.at[p2, quarter(q)], S_R, slot, (1 - c, own + core))
 
     def r_y_in(core):
@@ -155,9 +158,9 @@
             pl.when(off)(t_y(q).start)
     t_p(r).start()
 
-    lane32 = lax.broadcasted_iota(jnp.int32, (32, 128), 1)
-    lane40 = lax.broadcasted_iota(jnp.int32, (40, 128), 1)
-    lane16 = lax.broadcasted_iota(jnp.int32, (16, 128), 1)
+    lane32 = lax.broadcasted_iota(jnp.int32, (32, LANE), 1)
+    lane40 = lax.broadcasted_iota(jnp.int32, (HALF_V, LANE), 1)
+    lane16 = lax.broadcasted_iota(jnp.int32, (16, LANE), 1)
     vbuf[pl.ds(pl.multiple_of(1600 * (1 - k), 64), 64)] = jnp.zeros((64, COLS), BF16)
     wdp[:, pl.ds(VIRT, 48)] = jnp.zeros((OCC, 48, WIDE), BF16)
 
@@ -165,7 +168,7 @@
         @pl.loop(0, NCH)
         def _(g):
             parts = [
-                ref[half(h), pl.ds(pl.multiple_of(g * WIDE + 128 * m, 128), 128)].astype(F32)
+                ref[half(h), pl.ds(pl.multiple_of(g * WIDE + LANE * m, LANE), LANE)].astype(F32)
                 for m in range(5)
             ]
             for q, seg in enumerate(split_segments(parts, lane32)):
@@ -173,40 +176,40 @@
 
     def regroup(h, vh, l3_rows, tb_at):
         def rows(ik):
-            return zt[h, pl.ds(40 * ZS * vh + ik, 40, stride=ZS)]
+            return zt[h, pl.ds(HALF_V * ZS * vh + ik, HALF_V, stride=ZS)]
 
         @pl.loop(0, OCC)
         def _(kk):
             blk = jnp.concatenate([rows(kk), rows(OCC + kk)], axis=0).astype(BF16)
-            l3[l3_rows, pl.ds(pl.multiple_of(kk * 128, 128), 128)] = blk
-
-        for i in range(2):
+            l3[l3_rows, pl.ds(pl.multiple_of(kk * LANE, LANE), LANE)] = blk
+
+        for i in BOTH:
             @pl.loop(0, OCC // 2)
             def _(k2):
                 blk = jnp.concatenate([rows(i * OCC + 2 * k2), rows(i * OCC + 2 * k2 + 1)], axis=0).astype(BF16)
                 tb[tb_at + i, pl.ds(pl.multiple_of(k2 * VIRT, 16), VIRT)] = blk
 
     def r3(rows):
-        return jnp.dot(l3[rows], wdp[...].reshape(OCC * 128, WIDE), preferred_element_type=F32)
+        return jnp.dot(l3[rows], wdp[...].reshape(OCC * LANE, WIDE), preferred_element_type=F32)
 
     def r5(vh, first, count):
         rhs = jnp.concatenate([tb[first + i] for i in range(count)], axis=1)
         return lax.dot_general(wxs[vh], rhs, (((0,), (0,)), ((), ())), preferred_element_type=F32)
 
     def s_before():
-        for h in range(2):
+        for h in BOTH:
             slabs(tf, h, c)
         ld_wx.wait()
 
         @pl.loop(0, OCC // 2)
         def _(k2):
-            w = [wxb[2 * k2 + e].astype(F32) for e in range(2)]
+            w = [wxb[2 * k2 + e].astype(F32) for e in BOTH]
             at = pl.ds(pl.multiple_of(k2 * VIRT, 16), VIRT)
-            for vh in range(2):
-                part = [w[e][40 * vh:40 * vh + 40] for e in range(2)]
+            for vh in BOTH:
+                part = [w[e][HALF_V * vh:HALF_V * vh + 40] for e in BOTH]
                 wxs[vh, at] = jnp.concatenate(part, axis=0).astype(BF16)
 
-        for h in range(2):
+        for h in BOTH:
             regroup(h, c, pl.ds(VIRT * h, VIRT), 2 * h)
         ld_wd.wait()
         r3a[...] = r3(pl.ds(0, 2 * VIRT))
@@ -222,23 +225,23 @@
 
         @pl.loop(0, 2)
         def _(i):
-            rows_a = pl.ds(pl.multiple_of(VIRT * h + 40 * i, 8), 40)
-            rows_b = pl.ds(pl.multiple_of(40 * i, 8), 40)
-            seg_a = split_segments([r3a[rows_a, pl.ds(128 * m, 128)] for m in range(5)], lane40)
-            seg_b = split_segments([r3b[rows_b, pl.ds(128 * m, 128)] for m in range(5)], lane40)
-            lanes = pl.ds(pl.multiple_of(i * 128, 128), 128)
+            rows_a = pl.ds(pl.multiple_of(VIRT * h + HALF_V * i, 8), HALF_V)
+            rows_b = pl.ds(pl.multiple_of(HALF_V * i, 8), HALF_V)
+            seg_a = split_segments([r3a[rows_a, pl.ds(LANE * m, LANE)] for m in range(5)], lane40)
+            seg_b = split_segments([r3b[rows_b, pl.ds(LANE * m, LANE)] for m in range(5)], lane40)
+            lanes = pl.ds(pl.multiple_of(i * LANE, LANE), LANE)
             for j in range(8):
-                s_a = seg_a[j] - r5b[pl.ds(pl.multiple_of(j * VIRT + 40 * c, 8), 40), lanes]
-                s_b = seg_b[j] - r5b[pl.ds(pl.multiple_of(j * VIRT + 40 * (1 - c), 8), 40), lanes]
+                s_a = seg_a[j] - r5b[pl.ds(pl.multiple_of(j * VIRT + HALF_V * c, 8), HALF_V), lanes]
+                s_b = seg_b[j] - r5b[pl.ds(pl.multiple_of(j * VIRT + HALF_V * (1 - c), 8), HALF_V), lanes]
                 row = (j // 4) * 16 + (2 * h + i) * 4 + j % 4
-                zf[pl.ds(40 * ZS * c + row, 40, stride=ZS)] = s_a
-                zf[pl.ds(40 * ZS * (1 - c) + row, 40, stride=ZS)] = s_b
-                both = [jnp.where(c == 0, s_a, s_b), jnp.where(c == 0, s_b, s_a), jnp.zeros((48, 128), F32)]
+                zf[pl.ds(HALF_V * ZS * c + row, HALF_V, stride=ZS)] = s_a
+                zf[pl.ds(HALF_V * ZS * (1 - c) + row, HALF_V, stride=ZS)] = s_b
+                both = [jnp.where(c == 0, s_a, s_b), jnp.where(c == 0, s_b, s_a), jnp.zeros((48, LANE), F32)]
                 row = jnp.where(diag, j * 4 + 2 * h + i, h * 16 + j * 2 + i)
                 zg[pl.ds(row, VIRT, stride=ZS)] = jnp.transpose(jnp.concatenate(both, axis=0))[:VIRT]
 
     def tile_at(base, n, m):
-        return pl.ds(pl.multiple_of(base + n * WIDE + 128 * m, 128), 128)
+        return pl.ds(pl.multiple_of(base + n * WIDE + LANE * m, LANE), LANE)
 
     def slab(z, g, q, row, size):
         return z[pl.ds(pl.multiple_of((g * 8 + q) * ZS + row, 8), size)]
@@ -274,18 +277,17 @@
             for m, tile in enumerate(join_segments(segs, lane16)):
                 grecv[rows, tile_at(0, n, m)] = tile
 
-    def f_off(h, send):
-        lane8 = lax.broadcasted_iota(jnp.int32, (8, 128), 1)
+    def f_off(h, hf, first=0, last=NCH):
+        lane8 = lax.broadcasted_iota(jnp.int32, (8, LANE), 1)
         rows = pl.ds(8 * h, 8)
-        hf = 1 - c if send else c
-
-        @pl.loop(0, NCH)
+
+        @pl.loop(first, last)
         def _(n):
-            for b in range(2):
+            for b in BOTH:
                 segs = [slab(zf, n + NCH * hf, q, 16 * b + 8 * h, 8) for q in range(8)]
                 for m, tile in enumerate(join_segments(segs, lane8)):
                     fbuf[b, rows, tile_at(COLS * hf, n, m)] = tile
-            if send:
+            if hf is not c:
                 f_y(n, h).start()
 
     def g_p():
@@ -314,7 +316,7 @@
                     for m, tile in enumerate(join_segments(segs, lane16)):
                         fbuf[b, :, tile_at(COLS * hf, n, m)] = tile
                 if send:
-                    for h in range(2):
+                    for h in BOTH:
                         f_y(n, h).start()
 
         flat(1 - c, True)
@@ -329,7 +331,7 @@
         return rc(xp.at[p3, ts, hf, :, cols], prx.at[ts, hf, :, cols], S_PAIR, slot, d_p)
 
     def pair_e(n, h):
-        return pair(early, h, wide(n), E_D + h)
+        return pair(early, h, wide(n), E_D + 3 * h + n // 2)
 
     def pair_l(n, h):
         return pair(late, h, wide(n), L_D + h)
@@ -338,17 +340,10 @@
         ts = pl.ds(2 * h, 2)
         return rc(xp.at[p2, ts, hf, :, cols], xrecv.at[ts, hf, :, cols], S_X, slot, d_x)
 
-    def combine(hf, h, first, last, slot):
-        @pl.loop(first, last)
-        def _(n):
-            ts = pl.ds(2 * h, 2)
-            xp[p2, ts, hf, :, wide(n)] += prx[ts, hf, :, wide(n)]
-            cross(hf, h, wide(n), slot(n)).start()
-
     def over_columns(step):
         @pl.loop(0, 2)
         def _(g):
-            step(pl.ds(pl.multiple_of(g * 2 * WIDE, 128), 2 * WIDE), (2 * g, 2 * g + 1))
+            step(pl.ds(pl.multiple_of(g * 2 * WIDE, LANE), 2 * WIDE), (2 * g, 2 * g + 1))
 
         step(pl.ds(4 * WIDE, WIDE), (4,))
 
@@ -365,7 +360,7 @@
     def ladder_1():
         def step(cols, ns):
             lhs = jnp.concatenate(
-                [tr1[pl.ds(other, 2), half(1)].reshape(64, KPAD), tr1[pl.ds(own, 2)].reshape(128, KPAD)], axis=0
+                [tr1[pl.ds(other, 2), half(1)].reshape(64, KPAD), tr1[pl.ds(own, 2)].reshape(LANE, KPAD)], axis=0
             )
             prod = jnp.dot(lhs, vbuf[:, cols], preferred_element_type=F32)
             xp[pl.ds(other, 2), pl.ds(2, 2), :, :, cols] = prod[:64].reshape(2, 2, 2, 8, -1)
@@ -377,13 +372,23 @@
         over_columns(step)
 
     def combine_e(h):
-        pair(early, h, pl.ds(0, COLS), E_D + h).wait_recv()
-        combine(early, h, 0, NCH, lambda n: E_X)
-
-    def combine_l(h, first=0, last=NCH):
-        if first == 0:
-            pair(late, h, pl.ds(0, COLS), L_D + h).wait_recv()
-        combine(late, h, first, last, lambda n: L_X + 1 + n // 2 if h else L_X)
+        def step(cols, ns):
+            pair(early, h, cols, E_D + 3 * h + ns[0] // 2).wait_recv()
+            ts = pl.ds(2 * h, 2)
+            xp[p2, ts, early, :, cols] += prx[ts, early, :, cols]
+            cross(early, h, cols, E_X).start()
+
+        over_columns(step)
+
+    def combine_l(h):
+        pair(late, h, pl.ds(0, COLS), L_D + h).wait_recv()
+
+        def step(cols, ns):
+            ts = pl.ds(2 * h, 2)
+            xp[p2, ts, late, :, cols] += prx[ts, late, :, cols]
+            cross(late, h, cols, L_X + 1 + ns[0] // 2 if h else L_X).start()
+
+        over_columns(step)
 
     def out_pair(n):
         return rc(xp.at[p1, :, :, :, wide(n)], pown.at[:, :, :, wide(n)], S_OUT, O_D, d_p)
@@ -393,15 +398,15 @@
 
     def late_add(hs, wait_g):
         if wait_g:
-            for hh in range(2):
+            for hh in BOTH:
                 g_y_in(hh).wait_recv()
 
         @pl.loop(0, NCH)
         def _(n):
             for h in hs:
-                for b in range(2):
+                for b in BOTH:
                     for t in (2 * h, 2 * h + 1):
-                        g2 = [grecv[pl.ds(16 * hh + 8 * b + 2 * t, 2), wide(n)] for hh in range(2)]
+                        g2 = [grecv[pl.ds(16 * hh + 8 * b + 2 * t, 2), wide(n)] for hh in BOTH]
                         g8 = jnp.where(here, jnp.concatenate(g2 + g2, axis=0), 0.0)
                         xp[other + b, t, late, :, wide(n)] += g8
                 pair_l(n, h).start()
@@ -445,21 +450,21 @@
     def _():
         t_y(0).wait_recv()
         for cc in (1, 0):
-            r_x(cc).start()
+            r_x(0, cc).start()
+        t_x(0, p2).wait_recv()
+        t_fwd(0).start()
+        t_y(1).wait_recv()
+        r_x(1, k).start()
+        t_x(1, p2).wait_recv()
+        t_fwd(1).start()
+        r_y(1, 1 - k).start()
+        t_y(3).start()
         for q in range(2, 4):
             t_x(q, r).start()
-        t_x(0, p2).wait_recv()
-        t_fwd(0).start()
-        t_x(1, p2).wait_recv()
-        t_fwd(1).start()
-        for cc in (1, 0):
-            r_y(1, cc).start()
-        t_y(3).start()
         t_fwd_in(0).wait_recv()
         take(0)
         ld_v.wait()
         ladder_0()
-        t_y(1).wait_recv()
         s_prep(0)
         for q in range(2, 4):
             t_x(q, p2).wait_recv()
@@ -484,44 +489,45 @@
         q_diag()
         late_add((0, 1), True)
         combine_l(0)
-        combine_l(1, 0, 3)
         ld_oooo.wait()
         send_m()
-        combine_l(1, 3)
+        combine_l(1)
 
     @pl.when(off)
     def _():
-        for q in range(2):
+        for q in BOTH:
             t_y(q).wait_recv()
         s_prep(0)
         s_blocks(0)
         g_off(0)
-        for q in range(2):
+        for q in BOTH:
             t_x(q, p2).wait_recv()
             t_fwd(q).start()
+        f_off(0, 1 - c, 0, 3)
         ld_v.wait()
         for cc in (1, 0):
-            r_x(cc).wait_recv()
-            r_y(1, cc).wait_recv()
+            r_x(0, cc).wait_recv()
+        r_x(1, k).wait_recv()
+        r_y(1, 1 - k).wait_recv()
         ladder_0()
         t_y_in().wait_recv()
         r_p(r).start()
         tr1[r] = ty[:, my_k(k)]
         s_prep(1)
+        combine_e(0)
+        s_blocks(1)
         for q in range(2, 4):
             t_x(q, p2).wait_recv()
             t_fwd(q).start()
-        combine_e(0)
-        s_blocks(1)
         g_off(1)
         late_add((0,), False)
         t_p(p1).wait_recv()
-        for h in range(2):
+        for h in BOTH:
             t_fwd_in(h).wait_recv()
         ld_o.wait()
         x_part()
+        f_off(0, 1 - c, 3)
         combine_l(0)
-        f_off(0, True)
         for cc in (1, 0):
             r_y_in(cc).wait_recv()
         r_p(p1).wait_recv()
@@ -530,16 +536,16 @@
         ld_oooo.wait()
         send_m()
         combine_e(1)
-        f_off(1, True)
+        f_off(1, 1 - c)
         combine_l(1)
-        for h in range(2):
-            f_off(h, False)
+        for h in BOTH:
+            f_off(h, c)
 
     for cp in m_in():
         cp.wait_recv()
     ld_d.wait()
     rc(xp.at[p1], pown, S_OUT, O_D, d_p).wait_recv()
-    for h in range(2):
+    for h in BOTH:
         f_y_in(h).wait_recv()
     rc(xp.at[p2, :, x], xrecv.at[:, x], S_X, E_X, d_x).wait_recv()
     cross(1 - x, 0, pl.ds(0, COLS), L_X).wait_recv()
@@ -553,10 +559,10 @@
         )
         part = xp[r, :, :, :, cols] + pown[:, :, :, cols] + xrecv[:, :, :, cols]
         obuf[:, cols] = ov[:, cols].astype(F32) + r2 + part.reshape(ROWS, width)
-        mine = pl.ds(pl.multiple_of(COLS * c + ns[0] * WIDE, 128), width)
+        mine = pl.ds(pl.multiple_of(COLS * c + ns[0] * WIDE, LANE), width)
         for i in range(4):
             for ref, hf, at in ((fbuf, c, mine), (frecv, 1 - c, cols)):
-                f8 = jnp.concatenate([ref[b, pl.ds(4 * i, 4), at] for b in range(2)], axis=0)
+                f8 = jnp.concatenate([ref[b, pl.ds(4 * i, 4), at] for b in BOTH], axis=0)
                 rows = pl.ds(pl.multiple_of(16 * i + 8 * hf, 8), 8)
                 obuf[rows, cols] += f8
         obuf[:, cols] = obuf[:, cols] / dbuf[:, cols]
@@ -600,23 +606,23 @@
                 vm((ROWS, COLS), BF16),
                 vm((KPAD, COLS), BF16),
                 vm((ROWS, 256), BF16),
-                vm((OCC, 128, WIDE), BF16),
+                vm((OCC, LANE, WIDE), BF16),
                 vm((OCC, VIRT, WIDE), BF16),
                 vm((4, ROWS, COLS), BF16),
                 vm((ROWS, COLS), BF16),
                 vm((4, ROWS, KPAD), BF16),
-                vm((2, VIRT * ZS, 128), F32),
+                vm((2, VIRT * ZS, LANE), F32),
                 vm((2, WIDE, WIDE), BF16),
-                vm((4, WIDE, 128), BF16),
-                vm((2 * VIRT, OCC * 128), BF16),
+                vm((4, WIDE, LANE), BF16),
+                vm((2 * VIRT, OCC * LANE), BF16),
                 vm((2 * VIRT, WIDE), F32),
                 vm((VIRT, WIDE), F32),
                 vm((WIDE, 512), F32),
                 vm((WIDE, 256), F32),
-                vm((VIRT * ZS, 128), F32),
-                vm((VIRT * ZS, 128), F32),
-                vm((VIRT, 16, 128), F32),
-                vm((VIRT, 16, 128), F32),
+                vm((VIRT * ZS, LANE), F32),
+                vm((VIRT * ZS, LANE), F32),
+                vm((VIRT, 16, LANE), F32),
+                vm((VIRT, 16, LANE), F32),
                 vm((2, 16, 2 * COLS), F32),
                 vm((32, COLS), F32),
                 vm((2, 16, COLS), F32),

time: 40.5 us -> 39.4 us (0.973)
  Pallas kernels: 39.5 us -> 38.4 us
    pallas_call x1, Pallas kernels: 39.5 us -> 38.4 us  [sweep(): pl.pallas_call(kernel, out_shape=pltpu.VMEM((ROWS, COLS), F32), in_specs=...]
where the time goes in v6:
time: 39.4 us; the launch traced here: 39.3 us
  Pallas kernels  38.4 us (97%)
  local copies, waits for them, and re-layouts  0.89 us (2%)
    pallas_call x1, Pallas kernels, sweep(): pl.pallas_call(kernel, out_shape=pltpu.VMEM((ROWS, COLS), F32), in_specs=...  38.4 us
    unnamed x1, local copies, waits for them, and re-layouts  0.89 us

profile of v6, /device:TPU:0, one launch (start us, length us, event | category | flops | bytes accessed | tf_op | source)
XLA Modules:
  0.0 39.3 jit_solution(12166014437457569208)
XLA Ops:
  0.0 38.4 %ccd_sweep.1 = f32[64,3200]{1,0:T(8,128)S(1)} custom-call(f32[64,3200]{1,0:T(8,128)} %t_hbm.1, f32[64,3200]{1,0:T(8,128)} %d_hbm.1, bf16[64,3200]{1,0:T(8,128)(2,1)} %o_hbm.1, bf16[1600,3200]{1,0:T(8,128)(2,1)} %v_hbm.1, bf16[256,256]{1,0:T(8,128)(2,1)} %oooo_hbm.1, bf16[16,80,640]{2,1,0:T(8,128)(2,1)} %bitcast.2, bf16[16,80,640]{2,1,0:T(8,128)(2,1)} %bitcast.3), custom_call_target="tpu_custom_call" | custom-call | tf_op jit(solution)/shard_map/ccd_sweep/pallas_call | solution.py:598
  38.4 0.9 %copy.9 = f32[64,3200]{1,0:T(8,128)} copy(f32[64,3200]{1,0:T(8,128)S(1)} %ccd_sweep.1) | data formatting | bytes 1638400

commit v7 on v6

--- a/solution.py
+++ b/solution.py
@@ -24,10 +24,11 @@
 ZS = 40
 
 T_X, T_Y, T_P, T_FWD, R_P, G_P, R_X, R_Y, G_Y = 0, 4, 7, 8, 10, 10, 11, 13, 11
-E_D, L_D, O_D, E_X, L_X, F_Y, X_Y, M_1, M_2, M_3 = 17, 23, 25, 26, 27, 31, 33, 34, 35, 36
-N_RECV = 37
-S_TX, S_TY, S_TP, S_FWD, S_R, S_PAIR, S_OUT, S_X, S_F, S_G, S_XY, S_M = range(12)
-N_SEND = 12
+E_D, G_D, O_D, E_X, L_X, F_Y, X_Y, M_1, M_2, M_3 = 17, 23, 24, 25, 26, 30, 32, 33, 34, 35
+N_RECV = 36
+S_TX, S_TY, S_TP, S_FWD, S_R, S_PAIR, S_OUT, S_X, S_F, S_G, S_XY, S_M, S_GD = range(13)
+N_SEND = 13
+STEPS = (0, 1), (2, 3), (4,)
 
 
 def split_segments(parts, lane):
@@ -57,7 +58,7 @@
 def kernel(
     t_hbm, d_hbm, o_hbm, v_hbm, oooo_hbm, wd_hbm, wx_hbm, obuf,
     tf, dbuf, ov, vbuf, ob, wdp, wxb,
-    tcol, ty, tr1, zt, wxs, tb, l3, r3a, r3b, r5a, r5b, zf, zg, gps, gpz, fbuf, gbuf, frecv, grecv,
+    tcol, ty, tr1, zt, wxs, tb, l3, r3a, r3b, r5a, r5b, zf, zg, gps, gpz, fbuf, gbuf, gown, frecv, grecv,
     xp, prx, pown, xrecv, xpart, xyrecv, msend, mfull,
     lsem, ss, rs,
 ):
@@ -246,12 +247,17 @@
     def slab(z, g, q, row, size):
         return z[pl.ds(pl.multiple_of((g * 8 + q) * ZS + row, 8), size)]
 
-    def g_y(n, h):
-        rows = pl.ds(16 * h, 16)
-        return rc(gbuf.at[rows, wide(n)], grecv.at[rows, wide(n)], S_G, G_Y + h, d_y)
-
-    def g_y_in(h):
-        return rc(gbuf.at[pl.ds(16 * h, 16)], grecv.at[pl.ds(16 * h, 16)], S_G, G_Y + h, d_y)
+    def g_y(n, h, b):
+        return rc(gbuf.at[b, h, :, wide(n)], grecv.at[k, h, :, wide(n)], S_G, G_Y + k, (1 - c, own + b))
+
+    def g_y_in(core):
+        return rc(grecv.at[core], grecv.at[core], S_G, G_Y + core, d_y)
+
+    def g_d(h):
+        return rc(gown.at[1 - k, h], grecv.at[k, h], S_GD, G_D, d_p)
+
+    def g_d_in():
+        return rc(gown.at[1 - k], grecv.at[1 - k], S_GD, G_D, d_p)
 
     def f_y_in(h):
         rows = pl.ds(8 * h, 8)
@@ -262,20 +268,27 @@
         return rc(fbuf.at[:, rows, wide(n, COLS * (1 - c))], frecv.at[:, rows, wide(n)], S_F, F_Y + h, d_y)
 
     def g_off(h):
-        rows = pl.ds(16 * h, 16)
+        lane8 = lax.broadcasted_iota(jnp.int32, (8, LANE), 1)
+
+        def flat(dst, n, hf):
+            for b in BOTH:
+                segs = [slab(zg, n + NCH * hf, q, 16 * h + 8 * b, 8) for q in range(8)]
+                for m, tile in enumerate(join_segments(segs, lane8)):
+                    dst[b, h, :, tile_at(0, n, m)] = tile
 
         @pl.loop(0, NCH)
         def _(n):
-            segs = [slab(zg, n + NCH * (1 - c), q, 16 * h, 16) for q in range(8)]
-            for m, tile in enumerate(join_segments(segs, lane16)):
-                gbuf[rows, tile_at(0, n, m)] = tile
-            g_y(n, h).start()
+            flat(gown, n, c)
+
+        g_d(h).start()
 
         @pl.loop(0, NCH)
         def _(n):
-            segs = [slab(zg, n + NCH * c, q, 16 * h, 16) for q in range(8)]
-            for m, tile in enumerate(join_segments(segs, lane16)):
-                grecv[rows, tile_at(0, n, m)] = tile
+            flat(gbuf, n, 1 - c)
+            for b in BOTH:
+                g_y(n, h, b).start()
+
+        grecv[k, h] = gown[k, h]
 
     def f_off(h, hf, first=0, last=NCH):
         lane8 = lax.broadcasted_iota(jnp.int32, (8, LANE), 1)
@@ -326,15 +339,9 @@
 
     early, late = 1 - x, x
 
-    def pair(hf, h, cols, slot):
+    def pair(h, cols, step):
         ts = pl.ds(2 * h, 2)
-        return rc(xp.at[p3, ts, hf, :, cols], prx.at[ts, hf, :, cols], S_PAIR, slot, d_p)
-
-    def pair_e(n, h):
-        return pair(early, h, wide(n), E_D + 3 * h + n // 2)
-
-    def pair_l(n, h):
-        return pair(late, h, wide(n), L_D + h)
+        return rc(xp.at[p3, ts, :, :, cols], prx.at[ts, :, :, cols], S_PAIR, E_D + 3 * h + step, d_p)
 
     def cross(hf, h, cols, slot):
         ts = pl.ds(2 * h, 2)
@@ -352,8 +359,7 @@
             lhs = tr1[pl.ds(other, 2), half(0)].reshape(64, KPAD)
             prod = jnp.dot(lhs, vbuf[:, cols], preferred_element_type=F32)
             xp[pl.ds(other, 2), pl.ds(0, 2), :, :, cols] = prod.reshape(2, 2, 2, 8, -1)
-            for n in ns:
-                pair_e(n, 0).start()
+            pair(0, cols, ns[0] // 2).start()
 
         over_columns(step)
 
@@ -365,51 +371,28 @@
             prod = jnp.dot(lhs, vbuf[:, cols], preferred_element_type=F32)
             xp[pl.ds(other, 2), pl.ds(2, 2), :, :, cols] = prod[:64].reshape(2, 2, 2, 8, -1)
             xp[pl.ds(own, 2), :, :, :, cols] = prod[64:].reshape(2, 4, 2, 8, -1)
-            for n in ns:
-                pair_e(n, 1).start()
-                out_pair(n).start()
+            pair(1, cols, ns[0] // 2).start()
+            rc(xp.at[p1, :, :, :, cols], pown.at[:, :, :, cols], S_OUT, O_D, d_p).start()
 
         over_columns(step)
 
-    def combine_e(h):
+    def combine(h, first=0, last=3):
+        ts = pl.ds(2 * h, 2)
+        for step in range(first, last):
+            ns = STEPS[step]
+            cols = pl.ds(ns[0] * WIDE, len(ns) * WIDE)
+            pair(h, cols, step).wait_recv()
+            xp[p2, ts, :, :, cols] += prx[ts, :, :, cols]
+            cross(early, h, cols, E_X).start()
+
+    def late_pass(h):
         def step(cols, ns):
-            pair(early, h, cols, E_D + 3 * h + ns[0] // 2).wait_recv()
-            ts = pl.ds(2 * h, 2)
-            xp[p2, ts, early, :, cols] += prx[ts, early, :, cols]
-            cross(early, h, cols, E_X).start()
+            for t in (2 * h, 2 * h + 1):
+                g2 = [grecv[core, hh, pl.ds(2 * t, 2), cols] for core in BOTH for hh in BOTH]
+                xp[p2, t, late, :, cols] += jnp.concatenate(g2, axis=0)
+            cross(late, h, cols, L_X + 1 + ns[0] // 2 if h else L_X).start()
 
         over_columns(step)
-
-    def combine_l(h):
-        pair(late, h, pl.ds(0, COLS), L_D + h).wait_recv()
-
-        def step(cols, ns):
-            ts = pl.ds(2 * h, 2)
-            xp[p2, ts, late, :, cols] += prx[ts, late, :, cols]
-            cross(late, h, cols, L_X + 1 + ns[0] // 2 if h else L_X).start()
-
-        over_columns(step)
-
-    def out_pair(n):
-        return rc(xp.at[p1, :, :, :, wide(n)], pown.at[:, :, :, wide(n)], S_OUT, O_D, d_p)
-
-    row8 = lax.broadcasted_iota(jnp.int32, (8, WIDE), 0)
-    here = (row8 // 4) == k
-
-    def late_add(hs, wait_g):
-        if wait_g:
-            for hh in BOTH:
-                g_y_in(hh).wait_recv()
-
-        @pl.loop(0, NCH)
-        def _(n):
-            for h in hs:
-                for b in BOTH:
-                    for t in (2 * h, 2 * h + 1):
-                        g2 = [grecv[pl.ds(16 * hh + 8 * b + 2 * t, 2), wide(n)] for hh in BOTH]
-                        g8 = jnp.where(here, jnp.concatenate(g2 + g2, axis=0), 0.0)
-                        xp[other + b, t, late, :, wide(n)] += g8
-                pair_l(n, h).start()
 
     def x_y():
         return rc(xpart, xyrecv, S_XY, X_Y, d_y)
@@ -471,7 +454,7 @@
             t_fwd(q).start()
             for cc in (1, 0):
                 r_y(q, cc).start()
-        combine_e(0)
+        combine(0)
         s_blocks(0)
         t_p(p1).wait_recv()
         tr1[r] = tcol[r, :, my_k(k)]
@@ -481,17 +464,18 @@
         ladder_1()
         ld_o.wait()
         x_part()
-        combine_e(1)
+        combine(1)
         t_y_in().wait_recv()
         s_prep(1)
         s_blocks(1)
         give_g()
         q_diag()
-        late_add((0, 1), True)
-        combine_l(0)
+        for core in BOTH:
+            g_y_in(core).wait_recv()
+        late_pass(0)
         ld_oooo.wait()
         send_m()
-        combine_l(1)
+        late_pass(1)
 
     @pl.when(off)
     def _():
@@ -510,34 +494,34 @@
         r_x(1, k).wait_recv()
         r_y(1, 1 - k).wait_recv()
         ladder_0()
+        combine(0, 0, 1)
         t_y_in().wait_recv()
         r_p(r).start()
         tr1[r] = ty[:, my_k(k)]
         s_prep(1)
-        combine_e(0)
+        combine(0, 1)
         s_blocks(1)
         for q in range(2, 4):
             t_x(q, p2).wait_recv()
             t_fwd(q).start()
         g_off(1)
-        late_add((0,), False)
+        g_d_in().wait_recv()
+        late_pass(0)
+        for cc in (1, 0):
+            r_y_in(cc).wait_recv()
+        r_p(p1).wait_recv()
+        ladder_1()
         t_p(p1).wait_recv()
         for h in BOTH:
             t_fwd_in(h).wait_recv()
         ld_o.wait()
         x_part()
         f_off(0, 1 - c, 3)
-        combine_l(0)
-        for cc in (1, 0):
-            r_y_in(cc).wait_recv()
-        r_p(p1).wait_recv()
-        ladder_1()
-        late_add((1,), False)
         ld_oooo.wait()
         send_m()
-        combine_e(1)
+        combine(1)
+        late_pass(1)
         f_off(1, 1 - c)
-        combine_l(1)
         for h in BOTH:
             f_off(h, c)
 
@@ -589,6 +573,7 @@
     def _():
         r_p(r).wait_send()
         rc(gbuf, grecv, S_G, G_Y, d_y).wait_send()
+        g_d_in().wait_send()
 
 
 def solution(mesh):
@@ -624,9 +609,10 @@
                 vm((VIRT, 16, LANE), F32),
                 vm((VIRT, 16, LANE), F32),
                 vm((2, 16, 2 * COLS), F32),
-                vm((32, COLS), F32),
+                vm((2, 2, 8, COLS), F32),
+                vm((2, 2, 8, COLS), F32),
                 vm((2, 16, COLS), F32),
-                vm((32, COLS), F32),
+                vm((2, 2, 8, COLS), F32),
                 vm((4, 4, 2, 8, COLS), F32),
                 vm((4, 2, 8, COLS), F32),
                 vm((4, 2, 8, COLS), F32),

time: 39.4 us -> 38.6 us (0.980)
  Pallas kernels: 38.4 us -> 37.6 us
    pallas_call x1, Pallas kernels: 38.4 us -> 37.6 us  [sweep(): pl.pallas_call(kernel, out_shape=pltpu.VMEM((ROWS, COLS), F32), in_specs=...]
where the time goes in v7:
time: 38.6 us; the launch traced here: 38.5 us
  Pallas kernels  37.6 us (97%)
  local copies, waits for them, and re-layouts  0.89 us (2%)
    pallas_call x1, Pallas kernels, sweep(): pl.pallas_call(kernel, out_shape=pltpu.VMEM((ROWS, COLS), F32), in_specs=...  37.6 us
    unnamed x1, local copies, waits for them, and re-layouts  0.89 us

profile of v7, /device:TPU:0, one launch (start us, length us, event | category | flops | bytes accessed | tf_op | source)
XLA Modules:
  0.0 38.5 jit_solution(4752915026282583877)
XLA Ops:
  0.0 37.6 %ccd_sweep.1 = f32[64,3200]{1,0:T(8,128)S(1)} custom-call(f32[64,3200]{1,0:T(8,128)} %t_hbm.1, f32[64,3200]{1,0:T(8,128)} %d_hbm.1, bf16[64,3200]{1,0:T(8,128)(2,1)} %o_hbm.1, bf16[1600,3200]{1,0:T(8,128)(2,1)} %v_hbm.1, bf16[256,256]{1,0:T(8,128)(2,1)} %oooo_hbm.1, bf16[16,80,640]{2,1,0:T(8,128)(2,1)} %bitcast.2, bf16[16,80,640]{2,1,0:T(8,128)(2,1)} %bitcast.3), custom_call_target="tpu_custom_call" | custom-call | tf_op jit(solution)/shard_map/ccd_sweep/pallas_call | solution.py:583
  37.6 0.9 %copy.9 = f32[64,3200]{1,0:T(8,128)} copy(f32[64,3200]{1,0:T(8,128)S(1)} %ccd_sweep.1) | data formatting | bytes 1638400

commit v8 on v7

--- a/solution.py
+++ b/solution.py
@@ -144,11 +144,7 @@
         slot = R_Y + 2 + lax.rem(k + core, 2)
         return rc(tr1.at[p2, half(1)], tr1.at[p2, half(1)], S_R, slot, (1 - c, own + core))
 
-    for q in range(4):
-        ld_t(q).wait()
-        tcol[r, quarter(q)] = tf[quarter(q)].astype(BF16)
-        if q == 0:
-            pl.semaphore_wait(barrier, 5)
+    def send_t(q):
         if q < 2:
             t_x(q, r).start()
         else:
@@ -157,6 +153,18 @@
             t_y(q).start()
         else:
             pl.when(off)(t_y(q).start)
+
+    for q in range(4):
+        ld_t(q).wait()
+        tcol[r, quarter(q)] = tf[quarter(q)].astype(BF16)
+        if q == 0:
+            pl.semaphore_wait(barrier, 5)
+            send_t(q)
+        elif q == 1:
+            @pl.when(k == 0)
+            def _():
+                send_t(q)
+
     t_p(r).start()
 
     lane32 = lax.broadcasted_iota(jnp.int32, (32, LANE), 1)
@@ -212,9 +220,20 @@
 
         for h in BOTH:
             regroup(h, c, pl.ds(VIRT * h, VIRT), 2 * h)
+
+        @pl.when(k == 1)
+        def _():
+            for q in range(1, 4):
+                send_t(q)
+
         ld_wd.wait()
         r3a[...] = r3(pl.ds(0, 2 * VIRT))
         r5a[...] = r5(c, 0, 4)
+
+        @pl.when(k == 0)
+        def _():
+            for q in range(2, 4):
+                send_t(q)
 
     def s_prep(h):
         slabs(ty, h, 1 - c)
@@ -487,7 +506,7 @@
         for q in BOTH:
             t_x(q, p2).wait_recv()
             t_fwd(q).start()
-        f_off(0, 1 - c, 0, 3)
+        f_off(0, 1 - c, 0, 2)
         ld_v.wait()
         for cc in (1, 0):
             r_x(0, cc).wait_recv()
@@ -516,7 +535,7 @@
             t_fwd_in(h).wait_recv()
         ld_o.wait()
         x_part()
-        f_off(0, 1 - c, 3)
+        f_off(0, 1 - c, 2)
         ld_oooo.wait()
         send_m()
         combine(1)

time: 38.6 us -> 37.8 us (0.979)
  Pallas kernels: 37.6 us -> 36.9 us
    pallas_call x1, Pallas kernels: 37.6 us -> 36.9 us  [sweep(): pl.pallas_call(kernel, out_shape=pltpu.VMEM((ROWS, COLS), F32), in_specs=...]
where the time goes in v8:
time: 37.8 us
  Pallas kernels  36.9 us (98%)
  local copies, waits for them, and re-layouts  0.89 us (2%)
    pallas_call x1, Pallas kernels, sweep(): pl.pallas_call(kernel, out_shape=pltpu.VMEM((ROWS, COLS), F32), in_specs=...  36.9 us
    unnamed x1, local copies, waits for them, and re-layouts  0.89 us

profile of v8, /device:TPU:0, one launch (start us, length us, event | category | flops | bytes accessed | tf_op | source)
XLA Modules:
  0.0 37.8 jit_solution(13364139749696870255)
XLA Ops:
  0.0 36.9 %ccd_sweep.1 = f32[64,3200]{1,0:T(8,128)S(1)} custom-call(f32[64,3200]{1,0:T(8,128)} %t_hbm.1, f32[64,3200]{1,0:T(8,128)} %d_hbm.1, bf16[64,3200]{1,0:T(8,128)(2,1)} %o_hbm.1, bf16[1600,3200]{1,0:T(8,128)(2,1)} %v_hbm.1, bf16[256,256]{1,0:T(8,128)(2,1)} %oooo_hbm.1, bf16[16,80,640]{2,1,0:T(8,128)(2,1)} %bitcast.2, bf16[16,80,640]{2,1,0:T(8,128)(2,1)} %bitcast.3), custom_call_target="tpu_custom_call" | custom-call | tf_op jit(solution)/shard_map/ccd_sweep/pallas_call | solution.py:602
  36.9 0.9 %copy.9 = f32[64,3200]{1,0:T(8,128)} copy(f32[64,3200]{1,0:T(8,128)S(1)} %ccd_sweep.1) | data formatting | bytes 1638400

commit v9 on v8

--- a/solution.py
+++ b/solution.py
@@ -23,11 +23,11 @@
 NCH = COLS // WIDE
 ZS = 40
 
-T_X, T_Y, T_P, T_FWD, R_P, G_P, R_X, R_Y, G_Y = 0, 4, 7, 8, 10, 10, 11, 13, 11
-E_D, G_D, O_D, E_X, L_X, F_Y, X_Y, M_1, M_2, M_3 = 17, 23, 24, 25, 26, 30, 32, 33, 34, 35
-N_RECV = 36
-S_TX, S_TY, S_TP, S_FWD, S_R, S_PAIR, S_OUT, S_X, S_F, S_G, S_XY, S_M, S_GD = range(13)
-N_SEND = 13
+T_X, T_Y, T_P, T_FWD, R_P, G_P, R_0, R_1, G_Y = 0, 4, 7, 8, 10, 10, 11, 12, 11
+E_D, G_D, O_D, L_X, F_Y, X_Y, M_I = 13, 19, 20, 21, 25, 26, 27
+N_RECV = 28
+S_T, S_R, S_XP, S_F, S_G, S_XY, S_M, S_GD = range(8)
+N_SEND = 8
 STEPS = (0, 1), (2, 3), (4,)
 
 
@@ -109,22 +109,22 @@
         ld.start()
 
     def t_x(q, blk):
-        return rc(tcol.at[blk, quarter(q)], tcol.at[blk, quarter(q)], S_TX, T_X + q, d_x)
+        return rc(tcol.at[blk, quarter(q)], tcol.at[blk, quarter(q)], S_T, T_X + q, d_x)
 
     def t_y(q):
-        return rc(tcol.at[r, quarter(q)], ty.at[quarter(q)], S_TY, T_Y + min(q, 2), d_y)
+        return rc(tcol.at[r, quarter(q)], ty.at[quarter(q)], S_T, T_Y + min(q, 2), d_y)
 
     def t_y_in():
-        return rc(tcol.at[r, half(1)], ty.at[half(1)], S_TY, T_Y + 2, d_y)
+        return rc(tcol.at[r, half(1)], ty.at[half(1)], S_T, T_Y + 2, d_y)
 
     def t_fwd(q):
-        return rc(tcol.at[p2, quarter(q)], tcol.at[p2, quarter(q)], S_FWD, T_FWD + q // 2, d_p)
+        return rc(tcol.at[p2, quarter(q)], tcol.at[p2, quarter(q)], S_T, T_FWD + q // 2, d_p)
 
     def t_fwd_in(h):
-        return rc(tcol.at[p3, half(h)], tcol.at[p3, half(h)], S_FWD, T_FWD + h, d_p)
+        return rc(tcol.at[p3, half(h)], tcol.at[p3, half(h)], S_T, T_FWD + h, d_p)
 
     def t_p(blk):
-        return rc(tcol.at[blk], tcol.at[blk], S_TP, T_P, d_p)
+        return rc(tcol.at[blk], tcol.at[blk], S_T, T_P, d_p)
 
     def my_k(core):
         return pl.ds(pl.multiple_of(1536 * core, LANE), KPAD)
@@ -133,16 +133,14 @@
         return rc(ty.at[:, my_k(1 - k)], tr1.at[blk], S_R, R_P, d_p)
 
     def r_x(q, core):
-        slot = R_Y if q else R_X + lax.rem(k + core, 2)
-        return rc(ty.at[quarter(q), my_k(core)], tr1.at[r, quarter(q)], S_R, slot, (c, other + core))
+        return rc(ty.at[quarter(q), my_k(core)], tr1.at[r, quarter(q)], S_R, R_0, (c, other + core))
 
     def r_y(q, core):
-        slot = R_Y + 1 if q == 1 else R_Y + 2 + lax.rem(k + core, 2)
+        slot = R_0 if q == 1 else R_1
         return rc(tcol.at[p2, quarter(q), my_k(core)], tr1.at[p2, quarter(q)], S_R, slot, (1 - c, own + core))
 
-    def r_y_in(core):
-        slot = R_Y + 2 + lax.rem(k + core, 2)
-        return rc(tr1.at[p2, half(1)], tr1.at[p2, half(1)], S_R, slot, (1 - c, own + core))
+    def r_in(h, slot):
+        return rc(tr1.at[pl.ds(other, 2), half(h)], tr1.at[pl.ds(other, 2), half(h)], S_R, slot, d_y)
 
     def send_t(q):
         if q < 2:
@@ -267,10 +265,10 @@
         return z[pl.ds(pl.multiple_of((g * 8 + q) * ZS + row, 8), size)]
 
     def g_y(n, h, b):
-        return rc(gbuf.at[b, h, :, wide(n)], grecv.at[k, h, :, wide(n)], S_G, G_Y + k, (1 - c, own + b))
-
-    def g_y_in(core):
-        return rc(grecv.at[core], grecv.at[core], S_G, G_Y + core, d_y)
+        return rc(gbuf.at[b, h, :, wide(n)], grecv.at[k, h, :, wide(n)], S_G, G_Y, (1 - c, own + b))
+
+    def g_y_in():
+        return rc(grecv, grecv, S_G, G_Y, d_y)
 
     def g_d(h):
         return rc(gown.at[1 - k, h], grecv.at[k, h], S_GD, G_D, d_p)
@@ -278,13 +276,12 @@
     def g_d_in():
         return rc(gown.at[1 - k], grecv.at[1 - k], S_GD, G_D, d_p)
 
-    def f_y_in(h):
-        rows = pl.ds(8 * h, 8)
-        return rc(frecv.at[:, rows], frecv.at[:, rows], S_F, F_Y + h, d_y)
+    def f_y_in():
+        return rc(frecv, frecv, S_F, F_Y, d_y)
 
     def f_y(n, h):
         rows = pl.ds(8 * h, 8)
-        return rc(fbuf.at[:, rows, wide(n, COLS * (1 - c))], frecv.at[:, rows, wide(n)], S_F, F_Y + h, d_y)
+        return rc(fbuf.at[:, rows, wide(n, COLS * (1 - c))], frecv.at[:, rows, wide(n)], S_F, F_Y, d_y)
 
     def g_off(h):
         lane8 = lax.broadcasted_iota(jnp.int32, (8, LANE), 1)
@@ -360,11 +357,11 @@
 
     def pair(h, cols, step):
         ts = pl.ds(2 * h, 2)
-        return rc(xp.at[p3, ts, :, :, cols], prx.at[ts, :, :, cols], S_PAIR, E_D + 3 * h + step, d_p)
+        return rc(xp.at[p3, ts, :, :, cols], prx.at[ts, :, :, cols], S_XP, E_D + 3 * h + step, d_p)
 
     def cross(hf, h, cols, slot):
         ts = pl.ds(2 * h, 2)
-        return rc(xp.at[p2, ts, hf, :, cols], xrecv.at[ts, hf, :, cols], S_X, slot, d_x)
+        return rc(xp.at[p2, ts, hf, :, cols], xrecv.at[ts, hf, :, cols], S_XP, slot, d_x)
 
     def over_columns(step):
         @pl.loop(0, 2)
@@ -391,7 +388,7 @@
             xp[pl.ds(other, 2), pl.ds(2, 2), :, :, cols] = prod[:64].reshape(2, 2, 2, 8, -1)
             xp[pl.ds(own, 2), :, :, :, cols] = prod[64:].reshape(2, 4, 2, 8, -1)
             pair(1, cols, ns[0] // 2).start()
-            rc(xp.at[p1, :, :, :, cols], pown.at[:, :, :, cols], S_OUT, O_D, d_p).start()
+            rc(xp.at[p1, :, :, :, cols], pown.at[:, :, :, cols], S_XP, O_D, d_p).start()
 
         over_columns(step)
 
@@ -402,7 +399,7 @@
             cols = pl.ds(ns[0] * WIDE, len(ns) * WIDE)
             pair(h, cols, step).wait_recv()
             xp[p2, ts, :, :, cols] += prx[ts, :, :, cols]
-            cross(early, h, cols, E_X).start()
+            cross(early, h, cols, L_X).start()
 
     def late_pass(h):
         def step(cols, ns):
@@ -436,17 +433,13 @@
 
     def m_out():
         return (
-            rc(msend.at[p1], mfull.at[r], S_M, M_1, d_p),
-            rc(msend.at[p2], mfull.at[r], S_M, M_2, d_x),
-            rc(msend.at[p3], mfull.at[r], S_M, M_3, d_d),
+            rc(msend.at[p1], mfull.at[r], S_M, M_I, d_p),
+            rc(msend.at[p2], mfull.at[r], S_M, M_I, d_x),
+            rc(msend.at[p3], mfull.at[r], S_M, M_I, d_d),
         )
 
     def m_in():
-        return (
-            rc(msend.at[p1], mfull.at[p1], S_M, M_1, d_p),
-            rc(msend.at[p2], mfull.at[p2], S_M, M_2, d_x),
-            rc(msend.at[p3], mfull.at[p3], S_M, M_3, d_d),
-        )
+        return rc(mfull.at[pl.ds(0, 3)], mfull.at[pl.ds(0, 3)], S_M, M_I, d_p)
 
     @pl.when(diag)
     def _():
@@ -489,8 +482,7 @@
         s_blocks(1)
         give_g()
         q_diag()
-        for core in BOTH:
-            g_y_in(core).wait_recv()
+        g_y_in().wait_recv()
         late_pass(0)
         ld_oooo.wait()
         send_m()
@@ -508,10 +500,7 @@
             t_fwd(q).start()
         f_off(0, 1 - c, 0, 2)
         ld_v.wait()
-        for cc in (1, 0):
-            r_x(0, cc).wait_recv()
-        r_x(1, k).wait_recv()
-        r_y(1, 1 - k).wait_recv()
+        r_in(0, R_0).wait_recv()
         ladder_0()
         combine(0, 0, 1)
         t_y_in().wait_recv()
@@ -526,8 +515,7 @@
         g_off(1)
         g_d_in().wait_recv()
         late_pass(0)
-        for cc in (1, 0):
-            r_y_in(cc).wait_recv()
+        r_in(1, R_1).wait_recv()
         r_p(p1).wait_recv()
         ladder_1()
         t_p(p1).wait_recv()
@@ -544,23 +532,23 @@
         for h in BOTH:
             f_off(h, c)
 
-    for cp in m_in():
-        cp.wait_recv()
+    m_in().wait_recv()
     ld_d.wait()
-    rc(xp.at[p1], pown, S_OUT, O_D, d_p).wait_recv()
-    for h in BOTH:
-        f_y_in(h).wait_recv()
-    rc(xp.at[p2, :, x], xrecv.at[:, x], S_X, E_X, d_x).wait_recv()
-    cross(1 - x, 0, pl.ds(0, COLS), L_X).wait_recv()
-
-    def finish(cols, ns):
-        cross(1 - x, 1, cols, L_X + 1 + ns[0] // 2).wait_recv()
+    rc(xp.at[p1], pown, S_XP, O_D, d_p).wait_recv()
+    f_y_in().wait_recv()
+    rc(xp.at[p2, pl.ds(0, 3)], xrecv.at[pl.ds(0, 3)], S_XP, L_X, d_x).wait_recv()
+
+    def settle(t, hf, cols):
+        rows = pl.ds(pl.multiple_of(16 * t + 8 * hf, 8), 8)
+        obuf[rows, cols] = (obuf[rows, cols] + xrecv[t, hf, :, cols]) / dbuf[rows, cols]
+
+    def gather(cols, ns):
         width = len(ns) * WIDE
         r2 = lax.dot_general(
             mfull[...].reshape(4 * ROWS, ROWS), tcol[:, :, cols].reshape(4 * ROWS, width),
             (((0,), (0,)), ((), ())), preferred_element_type=F32,
         )
-        part = xp[r, :, :, :, cols] + pown[:, :, :, cols] + xrecv[:, :, :, cols]
+        part = xp[r, :, :, :, cols] + pown[:, :, :, cols]
         obuf[:, cols] = ov[:, cols].astype(F32) + r2 + part.reshape(ROWS, width)
         mine = pl.ds(pl.multiple_of(COLS * c + ns[0] * WIDE, LANE), width)
         for i in range(4):
@@ -568,25 +556,28 @@
                 f8 = jnp.concatenate([ref[b, pl.ds(4 * i, 4), at] for b in BOTH], axis=0)
                 rows = pl.ds(pl.multiple_of(16 * i + 8 * hf, 8), 8)
                 obuf[rows, cols] += f8
-        obuf[:, cols] = obuf[:, cols] / dbuf[:, cols]
-
+            settle(i, x, cols)
+            if i < 2:
+                settle(i, 1 - x, cols)
+
+    def finish(cols, ns):
+        cross(1 - x, 1, cols, L_X + 1 + ns[0] // 2).wait_recv()
+        for t in (2, 3):
+            settle(t, 1 - x, cols)
+
+    over_columns(gather)
     over_columns(finish)
 
-    rc(tcol.at[r], tcol.at[r], S_TX, T_X, d_x).wait_send()
-    rc(tcol.at[r], ty, S_TY, T_Y, d_y).wait_send()
-    rc(tcol.at[p2], tcol.at[p2], S_FWD, T_FWD, d_p).wait_send()
-    t_p(r).wait_send()
-    rc(xp.at[p3], prx, S_PAIR, E_D, d_p).wait_send()
-    rc(xp.at[p1], pown, S_OUT, O_D, d_p).wait_send()
-    rc(xp.at[p2], xrecv, S_X, E_X, d_x).wait_send()
+    rc(tcol, tcol, S_T, T_X, d_x).wait_send()
+    rc(xp.at[pl.ds(0, 3)], xp.at[pl.ds(0, 3)], S_XP, L_X, d_x).wait_send()
     rc(frecv, frecv, S_F, F_Y, d_y).wait_send()
     x_y().wait_send()
-    rc(msend.at[pl.ds(0, 3)], mfull.at[pl.ds(0, 3)], S_M, M_1, d_p).wait_send()
+    rc(msend.at[pl.ds(0, 3)], mfull.at[pl.ds(0, 3)], S_M, M_I, d_p).wait_send()
 
     @pl.when(diag)
     def _():
         g_p().wait_send()
-        rc(tr1.at[pl.ds(0, 2)], tr1.at[pl.ds(0, 2)], S_R, R_Y, d_y).wait_send()
+        rc(tr1.at[pl.ds(0, 2)], tr1.at[pl.ds(0, 2)], S_R, R_1, d_y).wait_send()
 
     @pl.when(off)
     def _():

time: 37.8 us -> 37.4 us (0.989)
  Pallas kernels: 36.9 us -> 36.5 us
    pallas_call x1, Pallas kernels: 36.9 us -> 36.5 us  [sweep(): pl.pallas_call(kernel, out_shape=pltpu.VMEM((ROWS, COLS), F32), in_specs=...]
where the time goes in v9:
time: 37.4 us
  Pallas kernels  36.5 us (98%)
  local copies, waits for them, and re-layouts  0.89 us (2%)
    pallas_call x1, Pallas kernels, sweep(): pl.pallas_call(kernel, out_shape=pltpu.VMEM((ROWS, COLS), F32), in_specs=...  36.5 us
    unnamed x1, local copies, waits for them, and re-layouts  0.89 us

profile of v9, /device:TPU:0, one launch (start us, length us, event | category | flops | bytes accessed | tf_op | source)
XLA Modules:
  0.0 37.4 jit_solution(11185032761098970446)
XLA Ops:
  0.0 36.5 %ccd_sweep.1 = f32[64,3200]{1,0:T(8,128)S(1)} custom-call(f32[64,3200]{1,0:T(8,128)} %t_hbm.1, f32[64,3200]{1,0:T(8,128)} %d_hbm.1, bf16[64,3200]{1,0:T(8,128)(2,1)} %o_hbm.1, bf16[1600,3200]{1,0:T(8,128)(2,1)} %v_hbm.1, bf16[256,256]{1,0:T(8,128)(2,1)} %oooo_hbm.1, bf16[16,80,640]{2,1,0:T(8,128)(2,1)} %bitcast.2, bf16[16,80,640]{2,1,0:T(8,128)(2,1)} %bitcast.3), custom_call_target="tpu_custom_call" | custom-call | tf_op jit(solution)/shard_map/ccd_sweep/pallas_call | solution.py:593
  36.5 0.9 %copy.9 = f32[64,3200]{1,0:T(8,128)} copy(f32[64,3200]{1,0:T(8,128)S(1)} %ccd_sweep.1) | data formatting | bytes 1638400
